TPU v7x, 32 devices: a whole 2x2x4 slice. The times are simulated.
32 devices in a mesh: dp: 2 (over x), cp: 4 (over z), tp: 4 (over y, core).
Axes of the slice: x: 2, y: 2, z: 4, core: 2. Of those that a mesh axis runs over, the one named last changes fastest.
Arguments:
- x: bfloat16 [8192, 3584], P(('dp', 'cp', 'tp')), parts along dimension 0
- idx: int32 [8192, 2], P(('dp', 'cp', 'tp')), parts along dimension 0
- gates: float32 [8192, 2], P(('dp', 'cp', 'tp')), parts along dimension 0
- wq: bfloat16 [3584, 3584], P(None, 'tp')
- wk: bfloat16 [3584, 512], P(None, 'tp')
- wv: bfloat16 [3584, 512], P(None, 'tp')
- wo: bfloat16 [3584, 3584], P('tp')
- w1g: bfloat16 [16, 3584, 2560], P(('cp', 'tp'))
- w1u: bfloat16 [16, 3584, 2560], P(('cp', 'tp'))
- w2: bfloat16 [16, 2560, 3584], P(('cp', 'tp'))
Outputs:
- output: bfloat16 [8192, 3584], P(('dp', 'cp', 'tp')), parts along dimension 0
There are 2 independent parts. A program takes and returns all parts, laid end to end along the dimension named above; an argument that names none is the same for every part.
All inputs are finite; a program needn't handle non-finite values.
Results may differ from a plain program's by a relative error of at most 0.0100627.
Values are sent between devices in bfloat16 or wider.
A program may use at most 1 GiB of HBM per device.

v0:
```python
import jax
import jax.numpy as jnp
from jax import lax
from jax.sharding import PartitionSpec as P

HEAD_DIM = 128
NEG = -1e30


def expert_ffn(rows, wg, wu, wd):
    gg = jnp.dot(rows, wg, preferred_element_type=jnp.float32)
    uu = jnp.dot(rows, wu, preferred_element_type=jnp.float32)
    act = (jax.nn.silu(gg) * uu).astype(jnp.bfloat16)
    return jnp.dot(act, wd, preferred_element_type=jnp.float32).astype(jnp.bfloat16)


def attention_residual(x, wq, wk, wv, wo, cp):
    rank = lax.axis_index('cp')
    xs = lax.all_gather(x, 'tp', axis=0, tiled=True)
    n = xs.shape[0]
    seg = n // 2
    q = jnp.dot(xs, wq, preferred_element_type=jnp.float32).astype(jnp.bfloat16)
    k = jnp.dot(xs, wk, preferred_element_type=jnp.float32).astype(jnp.bfloat16)
    v = jnp.dot(xs, wv, preferred_element_type=jnp.float32).astype(jnp.bfloat16)
    hq = q.shape[1] // HEAD_DIM
    hkvv = k.shape[1] // HEAD_DIM
    g = hq // hkvv
    kvs = lax.all_gather(jnp.concatenate([k, v], axis=1), 'cp', axis=0)
    rows = jnp.arange(n)

    def positions(src):
        s_id = jnp.where(rows < seg, src, 2 * cp - 1 - src)
        return s_id * seg + rows % seg

    qpos = positions(rank)
    q4 = q.reshape(n, hkvv, g, HEAD_DIM)
    scale = HEAD_DIM ** -0.5
    m = jnp.full((hkvv, g, n), NEG, jnp.float32)
    l = jnp.zeros((hkvv, g, n), jnp.float32)
    acc = jnp.zeros((hkvv, g, n, HEAD_DIM), jnp.float32)
    for j in range(cp):
        kj = kvs[j, :, :hkvv * HEAD_DIM].reshape(n, hkvv, HEAD_DIM)
        vj = kvs[j, :, hkvv * HEAD_DIM:].reshape(n, hkvv, HEAD_DIM)
        mask = positions(j)[None, :] <= qpos[:, None]
        s = jnp.einsum('nkgd,mkd->kgnm', q4, kj, preferred_element_type=jnp.float32) * scale
        s = jnp.where(mask, s, NEG)
        mn = jnp.maximum(m, jnp.max(s, axis=-1))
        w = jnp.where(mask, jnp.exp(s - mn[:, :, :, None]), 0.0)
        c = jnp.exp(m - mn)
        l = l * c + jnp.sum(w, axis=-1)
        acc = acc * c[:, :, :, None] + jnp.einsum('kgnm,mkd->kgnd', w.astype(jnp.bfloat16), vj, preferred_element_type=jnp.float32)
        m = mn
    o = (acc / l[:, :, :, None]).transpose(2, 0, 1, 3).reshape(n, hq * HEAD_DIM).astype(jnp.bfloat16)
    part = jnp.dot(o, wo, preferred_element_type=jnp.float32)
    att = lax.psum_scatter(part, 'tp', scatter_dimension=0, tiled=True)
    return (x.astype(jnp.float32) + att).astype(jnp.bfloat16)


def solution(mesh):
    cp = mesh.shape['cp']
    tp = mesh.shape['tp']
    ne = cp * tp
    rows_spec = P(('dp', 'cp', 'tp'), None)
    exp_spec = P(('cp', 'tp'), None, None)

    def local(x, idx, gates, wq, wk, wv, wo, w1g, w1u, w2):
        h = attention_residual(x, wq, wk, wv, wo, cp)
        t, hd = h.shape
        kk = idx.shape[1]
        cap = 4 * t // ne
        ea = idx.reshape(-1)
        tok = jnp.arange(t * kk) // kk
        onehot = (ea[:, None] == jnp.arange(ne)[None, :]).astype(jnp.int32)
        slot = jnp.take_along_axis(jnp.cumsum(onehot, axis=0), ea[:, None], axis=1)[:, 0] - 1
        send = jnp.zeros((ne, cap, hd), jnp.bfloat16).at[ea, slot].set(h[tok])
        recv = lax.all_to_all(send, ('cp', 'tp'), 0, 0, tiled=True)
        z = expert_ffn(recv.reshape(ne * cap, hd), w1g[0], w1u[0], w2[0])
        back = lax.all_to_all(z.reshape(ne, cap, hd), ('cp', 'tp'), 0, 0, tiled=True)
        zt = back[ea, slot].astype(jnp.float32).reshape(t, kk, hd)
        y = h.astype(jnp.float32) + jnp.sum(gates[:, :, None] * zt, axis=1)
        return y.astype(jnp.bfloat16)

    return jax.shard_map(local, mesh=mesh, in_specs=(rows_spec, rows_spec, rows_spec, P(None, 'tp'), P(None, 'tp'), P(None, 'tp'), P('tp', None), exp_spec, exp_spec, exp_spec), out_specs=rows_spec, check_vma=False)
```

profile of v0, /device:TPU:9, one launch (start us, length us, event | category | flops | bytes accessed | tf_op | source)
XLA Modules:
  0.0 1029.6 jit_solution(10203649637811199879)
XLA Ops:
  7.3 55.6 %all-gather.4.cloned.1.call-done = bf16[1024,3584]{1,0:T(8,128)(2,1)} async-done(((bf16[256,3584]{1,0:T(8,128)(2,1)}), bf16[1024,3584]{1,0:T(8,128)(2,1)}) %all-gather.4.cloned.1.call-update) | async-done | bytes 7340048 | tf_op jit(solution)/shard_map/all_gather | solution.py:19
  63.0 5.8 convolution_convert_fusion.1
  72.5 3.7 broadcast_compare_fusion.3
  76.1 11.0 %convolution_convert_fusion = bf16[1024,896]{0,1:T(8,128)(2,1)S(1)} fusion(bf16[1024,3584]{1,0:T(8,128)(2,1)} %all-gather.4.cloned.1.call-done, bf16[3584,896]{1,0:T(8,128)(2,1)} %param.13), kind=kOutput, calls=%fused_computation.52 | convolution fusion | flops 6577586176 | bytes 15597568 | tf_op jit(solution)/shard_map/dot_general | solution.py:22
  87.2 27.7 %all-gather.6.cloned.1.call-done = bf16[4096,256]{0,1:T(8,128)(2,1)} async-done(((bf16[1024,256]{0,1:T(8,128)(2,1)}), bf16[4096,256]{0,1:T(8,128)(2,1)}) %all-gather.6.cloned.1.call-update) | async-done | bytes 2097168 | tf_op jit(solution)/shard_map/all_gather | solution.py:28
  114.9 4.5 reshape.557
  119.4 8.7 fusion.88
  132.8 13.3 %fusion = (f32[7,1024]{1,0:T(8,128)S(1)}, f32[1024,1024,7]{1,0,2:T(8,128)}) fusion(pred[1024,1024]{0,1:T(8,128)(4,1)} %get-tuple-element.24, bf16[1024,7,128]{0,2,1:T(8,128)(2,1)S(1)} %bitcast.168, bf16[1,1024,128]{2,1,0:T(8,128)(2,1)} %copy.57), kind=kOutput, calls=%fused_computation.12 | convolution fusion | flops 1901061120 | bytes 32534528 | tf_op jit(solution)/shard_map/nkgd,mkd->kgnm/dot_general | solution.py:45
  146.1 12.3 %fusion.3 = (f32[7,1024]{1,0:T(8,128)S(1)}, f32[1024,1024,7]{1,0,2:T(8,128)}) fusion(pred[1024,1024]{0,1:T(8,128)(4,1)S(1)} %copy-done.3, bf16[1024,7,128]{0,2,1:T(8,128)(2,1)S(1)} %bitcast.169, bf16[1,1024,128]{2,1,0:T(8,128)(2,1)S(1)} %copy-done.9), kind=kOutput, calls=%fused_computation.15 | convolution fusion | flops 1901061120 | bytes 32534528 | tf_op jit(solution)/shard_map/nkgd,mkd->kgnm/dot_general | solution.py:45
  158.4 12.1 %fusion.2 = (f32[7,1024]{1,0:T(8,128)S(1)}, f32[1024,1024,7]{1,0,2:T(8,128)}) fusion(pred[1024,1024]{0,1:T(8,128)(4,1)S(1)} %copy-done.5, bf16[1024,7,128]{0,2,1:T(8,128)(2,1)S(1)} %bitcast.170, bf16[1,1024,128]{2,1,0:T(8,128)(2,1)S(1)} %copy.61), kind=kOutput, calls=%fused_computation.14 | convolution fusion | flops 1901061120 | bytes 32534528 | tf_op jit(solution)/shard_map/nkgd,mkd->kgnm/dot_general | solution.py:45
  170.6 12.1 %fusion.1 = (f32[7,1024]{1,0:T(8,128)S(1)}, f32[1024,1024,7]{1,0,2:T(8,128)}) fusion(pred[1024,1024]{0,1:T(8,128)(4,1)S(1)} %copy-done.6, bf16[1024,7,128]{0,2,1:T(8,128)(2,1)S(1)} %bitcast.171, bf16[1,1024,128]{2,1,0:T(8,128)(2,1)S(1)} %copy.59), kind=kOutput, calls=%fused_computation.13 | convolution fusion | flops 1901061120 | bytes 32534528 | tf_op jit(solution)/shard_map/nkgd,mkd->kgnm/dot_general | solution.py:45
  182.7 15.7 %fusion.22 = f32[7,1024,128]{1,2,0:T(8,128)} fusion(f32[1024,1024,7]{1,0,2:T(8,128)} %get-tuple-element.35, f32[7,1024]{1,0:T(8,128)S(1)} %get-tuple-element.23, pred[1024,1024]{0,1:T(8,128)(4,1)S(1)} %copy-done.7, bf16[1,1024,128]{1,0,2:T(2,128)(2,1)S(1)} %copy-done.14), kind=kOutput, calls=%fused_computation.34 | convolution fusion | flops 1915748352 | bytes 34369536 | tf_op jit(solution)/shard_map/kgnm,mkd->kgnd/dot_general | solution.py:51
  198.4 22.8 %fusion.4 = (f32[7,1024]{1,0:T(8,128)S(1)}, f32[7,1024]{1,0:T(8,128)S(1)}) fusion(f32[1024,1024,7]{1,0,2:T(8,128)} %get-tuple-element.35, f32[7,1024]{1,0:T(8,128)S(1)} %get-tuple-element.23, pred[1024,1024]{0,1:T(8,128)(4,1)S(1)} %copy-done.7, f32[7,1024]{1,0:T(8,128)S(1)} %get-tuple-element.11, f32[1024,1024,7]{1,0,2:T(8,128)} %get-tuple-element.33, ...), kind=kLoop, calls=%fused_computation.16 | loop fusion | flops 73385984 | bytes 60932096 | tf_op jit(solution)/shard_map/reduce_sum | solution.py:50
  221.2 15.8 %fusion.24 = f32[7,1024,128]{1,2,0:T(8,128)} fusion(f32[1024,1024,7]{1,0,2:T(8,128)} %get-tuple-element.33, f32[7,1024]{1,0:T(8,128)S(1)} %get-tuple-element.11, pred[1024,1024]{0,1:T(8,128)(4,1)S(1)} %copy-done.6, bf16[1,1024,128]{1,0,2:T(2,128)(2,1)S(1)} %copy-done.13), kind=kOutput, calls=%fused_computation.35 | convolution fusion | flops 1915748352 | bytes 34369536 | tf_op jit(solution)/shard_map/kgnm,mkd->kgnd/dot_general | solution.py:51
  237.0 15.8 %fusion.26 = f32[7,1024,128]{1,2,0:T(8,128)} fusion(f32[1024,1024,7]{1,0,2:T(8,128)} %get-tuple-element.31, f32[7,1024]{1,0:T(8,128)S(1)} %get-tuple-element.10, pred[1024,1024]{0,1:T(8,128)(4,1)S(1)} %copy-done.5, bf16[1,1024,128]{1,0,2:T(2,128)(2,1)S(1)} %copy-done.12), kind=kOutput, calls=%fused_computation.36 | convolution fusion | flops 1915748352 | bytes 34369536 | tf_op jit(solution)/shard_map/kgnm,mkd->kgnd/dot_general | solution.py:51
  252.8 22.5 %fusion.8 = (f32[7,1024]{1,0:T(8,128)S(1)}, f32[7,1024]{1,0:T(8,128)S(1)}) fusion(f32[1024,1024,7]{1,0,2:T(8,128)} %get-tuple-element.31, f32[7,1024]{1,0:T(8,128)S(1)} %get-tuple-element.10, pred[1024,1024]{0,1:T(8,128)(4,1)S(1)} %copy-done.5, f32[7,1024]{1,0:T(8,128)S(1)} %get-tuple-element.9, f32[1024,1024,7]{1,0,2:T(8,128)} %get-tuple-element.29, ...), kind=kLoop, calls=%fused_computation.20 | loop fusion | flops 73385984 | bytes 60932096 | tf_op jit(solution)/shard_map/reduce_sum | solution.py:50
  275.3 18.5 %divide_convert_fusion = bf16[7,1024,128]{1,2,0:T(8,128)(2,1)} fusion(f32[7,1024,128]{1,2,0:T(8,128)} %fusion.26, f32[7,1024,128]{1,2,0:T(8,128)} %fusion.24, f32[7,1024,128]{1,2,0:T(8,128)} %fusion.22, f32[1024,1024,7]{1,0,2:T(8,128)} %get-tuple-element.29, f32[7,1024]{1,0:T(8,128)S(1)} %get-tuple-element.9, pred[1024,1024]{0,1:T(8,128)(4,1)S(1)} %copy-done.4, ...), kind=kOutput, calls=%fused_computation.47 | convolution fusion | flops 1924005888 | bytes 43687936 | tf_op jit(solution)/shard_map/kgnm,mkd->kgnd/dot_general | solution.py:51
  293.8 14.2 %fusion.89 = f32[1024,3584]{1,0:T(8,128)} fusion(bf16[1024,896]{0,1:T(8,128)(2,1)} %bitcast.180, bf16[896,3584]{1,0:T(8,128)(2,1)} %param.16), kind=kOutput, calls=%fused_computation.135 | convolution fusion | flops 6576668672 | bytes 22937600 | tf_op jit(solution)/shard_map/dot_general | solution.py:54
  310.8 4.5 gather_fusion.2
  315.4 102.7 %reduce-scatter.2.cloned.1.call-done = f32[256,3584]{1,0:T(8,128)} async-done(((f32[1024,3584]{1,0:T(8,128)}), f32[256,3584]{1,0:T(8,128)}) %reduce-scatter.2.cloned.1.call-update) | async-done | bytes 3670032 | tf_op jit(solution)/shard_map/reduce_scatter | solution.py:55
  421.1 4.2 gather_fusion
  425.3 3.7 broadcast_in_dim.120
  429.0 122.1 %scatter_fusion = bf16[16,64,3584]{2,1,0:T(8,128)(2,1)} fusion(bf16[16,64,3584]{2,1,0:T(8,128)(2,1)} %broadcast_in_dim.120, s32[512]{0:T(512)S(1)} %bitcast.173, bf16[512,3584]{1,0:T(8,128)(2,1)} %gather_fusion), kind=kCustom, calls=%fused_computation.3 | custom fusion | bytes 11014144 | tf_op jit(solution)/shard_map/scatter | solution.py:75
  551.1 165.0 %all_to_all.10 = bf16[16,64,3584]{2,1,0:T(8,128)(2,1)S(1)} all-to-all(bf16[16,64,3584]{2,1,0:T(8,128)(2,1)} %scatter_fusion), channel_id=1, replica_groups=mesh['dp'=2,'cp'=4,'tp'=4] {'cp','tp'}, dimensions={0} | all-to-all | bytes 14680064 | tf_op jit(solution)/shard_map/all_to_all | solution.py:76
  719.1 23.2 %fusion.16 = f32[1024,2560]{1,0:T(8,128)} fusion(bf16[1024,3584]{1,0:T(8,128)(2,1)S(1)} %bitcast.176, bf16[1,3584,2560]{2,1,0:T(8,128)(2,1)} %param.17), kind=kOutput, calls=%fused_computation.28 | convolution fusion | flops 18790481920 | bytes 36175872 | tf_op jit(solution)/shard_map/dot_general | solution.py:11
  742.3 28.5 %multiply_convert_fusion = bf16[1024,2560]{1,0:T(8,128)(2,1)} fusion(f32[1024,2560]{1,0:T(8,128)} %fusion.16, bf16[1024,3584]{1,0:T(8,128)(2,1)} %bitcast.177, bf16[1,3584,2560]{2,1,0:T(8,128)(2,1)} %param.18), kind=kOutput, calls=%fused_computation.42 | convolution fusion | flops 18806210560 | bytes 41418752 | tf_op jit(solution)/shard_map/dot_general | solution.py:12
  770.8 26.5 %fusion.34 = bf16[1024,3584]{1,0:T(8,128)(2,1)} fusion(bf16[1024,2560]{1,0:T(8,128)(2,1)} %multiply_convert_fusion, bf16[1,2560,3584]{2,1,0:T(8,128)(2,1)} %param.19), kind=kOutput, calls=%fused_computation.43 | convolution fusion | flops 18794151936 | bytes 30932992 | tf_op jit(solution)/shard_map/dot_general | solution.py:14
  797.3 6.2 all-to-all-start.1
  803.7 156.8 %all-to-all-done.1 = bf16[16,64,3584]{2,1,0:T(8,128)(2,1)} async-done(((bf16[16,64,3584]{2,1,0:T(8,128)(2,1)}), bf16[16,64,3584]{2,1,0:T(8,128)(2,1)}, u32[]{:S(2)}, u32[]{:S(2)}) %all-to-all-start.1) | async-done | bytes 7340064 | tf_op jit(solution)/shard_map/all_to_all | solution.py:78
  960.5 16.4 %gather_fusion.1 = bf16[512,3584]{1,0:T(8,128)(2,1)} fusion(bf16[16,64,3584]{2,1,0:T(8,128)(2,1)} %all-to-all-done.1, s32[512]{0:T(512)S(1)} %bitcast.172), kind=kCustom, calls=%fused_computation.1 | custom fusion | bytes 7344128 | tf_op jit(solution)/shard_map/gather | solution.py:79
  976.9 8.7 reshape.528
  985.6 35.3 %multiply_reduce_fusion = f32[256,3584]{1,0:T(8,128)S(1)} fusion(f32[256,2,3584]{2,1,0:T(2,128)} %reshape.528, f32[256,2]{1,0:T(8,128)S(1)} %copy.44), kind=kLoop, calls=%fused_computation.44 | loop fusion | flops 2752512 | bytes 11012096 | tf_op jit(solution)/shard_map/reduce_sum | solution.py:80
  (73 shorter events, 19.7 us)
Async XLA Ops:
  6.5 56.4 %copy-start = (bf16[3584,128]{1,0:T(8,128)(2,1)S(1)}, bf16[3584,128]{1,0:T(8,128)(2,1)}, u32[]{:S(2)}) copy-start(bf16[3584,128]{1,0:T(8,128)(2,1)} %param.15) | copy-start | bytes 2752516
  6.5 62.2 %copy-start.10 = (bf16[3584,128]{1,0:T(8,128)(2,1)S(1)}, bf16[3584,128]{1,0:T(8,128)(2,1)}, u32[]{:S(2)}) copy-start(bf16[3584,128]{1,0:T(8,128)(2,1)} %param.14) | copy-start | bytes 2752516
  6.5 56.4 %all-gather.4.cloned.1.call-start = ((), (), s32[]{:S(2)}) async-start(), calls=%async_computation.3 | async-start | bytes 9175040 | tf_op jit(solution)/shard_map/all_gather | solution.py:19
  7.3 107.6 %all-gather.6.cloned.1.call-start = ((), (), s32[]{:S(2)}) async-start(), calls=%async_computation.5 | async-start | bytes 2621440 | tf_op jit(solution)/shard_map/all_gather | solution.py:28
  63.0 5.8 copy-start.2
  72.2 346.0 %reduce-scatter.2.cloned.1.call-start = ((), (), s32[]{:S(2)}) async-start(), calls=%async_computation.4 | async-start | bytes 18350080 | tf_op jit(solution)/shard_map/reduce_scatter | solution.py:55
  132.8 13.3 %copy-start.3 = (pred[1024,1024]{0,1:T(8,128)(4,1)S(1)}, pred[1024,1024]{0,1:T(8,128)(4,1)}, u32[]{:S(2)}) copy-start(pred[1024,1024]{0,1:T(8,128)(4,1)} %get-tuple-element.27) | copy-start | bytes 3145732
  132.8 13.3 %copy-start.9 = (bf16[1,1024,128]{2,1,0:T(8,128)(2,1)S(1)}, bf16[1,1024,128]{2,1,0:T(8,128)(2,1)}, u32[]{:S(2)}) copy-start(bf16[1,1024,128]{2,1,0:T(8,128)(2,1)} %copy.63) | copy-start | bytes 786436
  146.1 12.3 %copy-start.5 = (pred[1024,1024]{0,1:T(8,128)(4,1)S(1)}, pred[1024,1024]{0,1:T(8,128)(4,1)}, u32[]{:S(2)}) copy-start(pred[1024,1024]{0,1:T(8,128)(4,1)} %get-tuple-element.26) | copy-start | bytes 3145732
  158.4 12.1 %copy-start.6 = (pred[1024,1024]{0,1:T(8,128)(4,1)S(1)}, pred[1024,1024]{0,1:T(8,128)(4,1)}, u32[]{:S(2)}) copy-start(pred[1024,1024]{0,1:T(8,128)(4,1)} %get-tuple-element.25) | copy-start | bytes 3145732
  170.5 12.1 %copy-start.7 = (pred[1024,1024]{0,1:T(8,128)(4,1)S(1)}, pred[1024,1024]{0,1:T(8,128)(4,1)}, u32[]{:S(2)}) copy-start(pred[1024,1024]{0,1:T(8,128)(4,1)} %get-tuple-element.24) | copy-start | bytes 3145732
  170.5 12.1 %copy-start.14 = (bf16[1,1024,128]{1,0,2:T(2,128)(2,1)S(1)}, bf16[1,1024,128]{1,0,2:T(2,128)(2,1)}, u32[]{:S(2)}) copy-start(bf16[1,1024,128]{1,0,2:T(2,128)(2,1)} %get-tuple-element.19) | copy-start | bytes 786436
  198.4 22.8 %copy-start.13 = (bf16[1,1024,128]{1,0,2:T(2,128)(2,1)S(1)}, bf16[1,1024,128]{1,0,2:T(2,128)(2,1)}, u32[]{:S(2)}) copy-start(bf16[1,1024,128]{1,0,2:T(2,128)(2,1)} %get-tuple-element.17) | copy-start | bytes 786436
  221.2 15.8 %copy-start.12 = (bf16[1,1024,128]{1,0,2:T(2,128)(2,1)S(1)}, bf16[1,1024,128]{1,0,2:T(2,128)(2,1)}, u32[]{:S(2)}) copy-start(bf16[1,1024,128]{1,0,2:T(2,128)(2,1)} %get-tuple-element.15) | copy-start | bytes 786436
  252.8 22.5 %copy-start.4 = (pred[1024,1024]{0,1:T(8,128)(4,1)S(1)}, pred[1024,1024]{0,1:T(8,128)(4,1)}, u32[]{:S(2)}) copy-start(pred[1024,1024]{0,1:T(8,128)(4,1)} %get-tuple-element.27) | copy-start | bytes 3145732
  252.8 22.5 %copy-start.11 = (bf16[1,1024,128]{1,0,2:T(2,128)(2,1)S(1)}, bf16[1,1024,128]{1,0,2:T(2,128)(2,1)}, u32[]{:S(2)}) copy-start(bf16[1,1024,128]{1,0,2:T(2,128)(2,1)} %get-tuple-element.14) | copy-start | bytes 786436
  308.0 0.7 copy-start.15
  716.1 3.0 copy-start.8
  797.3 6.3 copy-start.16
  797.3 163.2 %all-to-all-start.1 = ((bf16[16,64,3584]{2,1,0:T(8,128)(2,1)}), bf16[16,64,3584]{2,1,0:T(8,128)(2,1)}, u32[]{:S(2)}, u32[]{:S(2)}) async-start(bf16[16,64,3584]{2,1,0:T(8,128)(2,1)} %bitcast.175), calls=%async_computation.2 | async-start | bytes 14680064 | tf_op jit(solution)/shard_map/all_to_all | solution.py:78
  976.9 45.7 %copy-start.1 = (bf16[3584,128]{1,0:T(8,128)(2,1)S(1)}, bf16[3584,128]{1,0:T(8,128)(2,1)}, u32[]{:S(2)}) copy-start(bf16[3584,128]{1,0:T(8,128)(2,1)} %param.15) | copy-start | bytes 2752516
Sparse Core Ops, SparseCore 0:
  8.9 54.0 all-gather.3
  72.3 42.5 all-gather.5
  308.2 109.8 reduce-scatter.1
where the time goes:
time: 1040 us; the launch traced here: 1030 us
  waiting for transfers between devices  344 us (33%)
  matrix products  227 us (22%)
  local copies, waits for them, and re-layouts  182 us (18%)
  blocking collectives  165 us (16%)
  other arithmetic  91.2 us (9%)
  between operations  13.9 us (1%)
    all_to_all x1, blocking collectives, local(): recv = lax.all_to_all(send, ('cp', 'tp'), 0, 0, tiled=True)  165 us
    all_to_all x1, waiting for transfers between devices, local(): lax.all_to_all(z.reshape(ne, cap, hd), ('cp', 'tp'), 0, 0, tiled=True)  157 us
    scatter x1, local copies, waits for them, and re-layouts, local(): send = jnp.zeros((ne, cap, hd), jnp.bfloat16).at[ea, slot].set(h[tok])  122 us
    reduce_scatter x1, waiting for transfers between devices, attention_residual(): att = lax.psum_scatter(part, 'tp', scatter_dimension=0, tiled=True)  103 us
    dot_general x4, matrix products, attention_residual(): jnp.einsum('kgnm,mkd->kgnd', w.astype(jnp.bfloat16), vj, preferred_elemen...  65.8 us
    all_gather x1, waiting for transfers between devices, attention_residual(): xs = lax.all_gather(x, 'tp', axis=0, tiled=True)  55.6 us
    dot_general x4, matrix products, attention_residual(): jnp.einsum('nkgd,mkd->kgnm', q4, kj, preferred_element_type=jnp.float32)  49.8 us
    reduce_sum x2, other arithmetic, attention_residual(): l = l * c + jnp.sum(w, axis=-1)  45.3 us
  transfers between devices with their start and end apart: 4, of which 4 were waited for; matrix products, arithmetic and copies ran while one was open for 2% of the time, Pallas kernels for 0%

commit v1 on v0

v1 whole, which is shorter than its diff:
```python
import functools

import jax
import jax.numpy as jnp
from jax import lax
from jax.experimental import pallas as pl
from jax.experimental.pallas import tpu as pltpu
from jax.sharding import PartitionSpec as P

HD = 128
NEG = -1e30
BF = jnp.bfloat16
F32 = jnp.float32
MESH = pl.DeviceIdType.MESH
VMEM_LIMIT = 67_000_000
CH = 16


def dot(a, b):
    return jnp.dot(a, b, preferred_element_type=F32)


def flash_kernel(q_ref, k_ref, v_ref, o_ref, vt_ref, *, seg, ncp, scale):
    c = lax.axis_index("cp")
    last = 2 * ncp - 1

    @pl.when(pl.program_id(0) == 0)
    def _():
        for b in range(2 * ncp):
            vt_ref[:, b * seg:(b + 1) * seg] = v_ref[b * seg:(b + 1) * seg, :].T

    def place(g):
        r = jnp.minimum(g, last - g)
        return pl.multiple_of((2 * r + jnp.where(g == r, 0, 1)) * seg, seg)

    def step(g, carry, qb, masked):
        m, l, acc = carry
        at = place(g)
        s = lax.dot_general(k_ref[pl.ds(at, seg), :], qb, (((1,), (1,)), ((), ())), preferred_element_type=F32) * scale
        if masked:
            ki = lax.broadcasted_iota(jnp.int32, s.shape, 0)
            qi = lax.broadcasted_iota(jnp.int32, s.shape, 1)
            s = jnp.where(ki <= qi, s, NEG)
        mn = jnp.maximum(m, jnp.max(s, axis=0, keepdims=True))
        w = jnp.exp(s - mn)
        a = jnp.exp(m - mn)
        l = l * a + jnp.sum(w, axis=0, keepdims=True)
        acc = acc * a + dot(vt_ref[:, pl.ds(at, seg)], w.astype(BF))
        return mn, l, acc

    for half in range(2):
        mine = c if half == 0 else last - c
        qb = q_ref[half * seg:(half + 1) * seg, :]
        carry = (jnp.full((1, seg), NEG, F32), jnp.zeros((1, seg), F32), jnp.zeros((HD, seg), F32))
        carry = lax.fori_loop(0, mine, lambda g, cr: step(g, cr, qb, False), carry)
        m, l, acc = step(mine, carry, qb, True)
        o_ref[half * seg:(half + 1) * seg, :] = (acc / l).T.astype(BF)


def flash(q, k, v, ncp):
    n, d = q.shape
    heads = d // HD
    kern = functools.partial(flash_kernel, seg=n // 2, ncp=ncp, scale=HD ** -0.5)
    full = pl.BlockSpec(k.shape, lambda h: (0, 0))
    return pl.pallas_call(
        kern,
        grid=(heads,),
        in_specs=[pl.BlockSpec((n, HD), lambda h: (0, h)), full, full],
        out_specs=pl.BlockSpec((n, HD), lambda h: (0, h)),
        out_shape=jax.ShapeDtypeStruct((n, d), BF),
        scratch_shapes=[pltpu.VMEM((HD, k.shape[0]), BF)],
        compiler_params=pltpu.CompilerParams(vmem_limit_bytes=VMEM_LIMIT, dimension_semantics=("arbitrary",)),
        name="flash",
        cost_estimate=pl.CostEstimate(flops=heads * n * k.shape[0] * HD * 2, bytes_accessed=4 * n * d, transcendentals=heads * n * k.shape[0] // 2),
    )(q, k, v)


def moe_kernel(h_ref, dr_ref, dc_ref, g_ref, wg_hbm, wu_hbm, wd_hbm, y_ref,
               send, recv, zbuf, back, act, w1buf, w2buf,
               ssem, rsem, zsem, bsem, w1sem, w2sem, *, ncp, ntp, nch, f1, f2):
    ne = ncp * ntp
    rows = ne * CH
    t, hd = h_ref.shape
    ff = wg_hbm.shape[1]
    n1, n2 = ff // f1, hd // f2
    r1, r2 = w1buf.shape[0], w2buf.shape[0]
    dp = lax.axis_index("dp")
    c = lax.axis_index("cp")
    p = lax.axis_index("tp")
    me = c * ntp + p

    order = [2, 1, 3, 0]
    peers = [(dc, dt) for dc in order[:ncp] for dt in range(ntp) if (dc, dt) != (0, 0)]

    def peer(dc, dt):
        pc = lax.rem(c + dc, ncp)
        pt = lax.rem(p + dt, ntp)
        return pc, pt, pc * ntp + pt

    def blk(e):
        return pl.ds(pl.multiple_of(e * CH, CH), CH)

    def out_copy(j, dc, dt):
        pc, pt, e = peer(dc, dt)
        return pltpu.make_async_remote_copy(send.at[j, blk(e)], recv.at[j, blk(me)], ssem.at[j, e], rsem.at[j, me],
                                            device_id=(dp, pc, pt), device_id_type=MESH)

    def in_copy(j, dc, dt):
        pc, pt, e = peer(dc, dt)
        return pltpu.make_async_remote_copy(send.at[j, blk(e)], recv.at[j, blk(e)], ssem.at[j, e], rsem.at[j, e],
                                            device_id=(dp, pc, pt), device_id_type=MESH)

    def home_copy(j, dc, dt):
        pc, pt, e = peer(dc, dt)
        return pltpu.make_async_remote_copy(zbuf.at[j, blk(e)], back.at[j, blk(me)], zsem.at[j, e], bsem.at[j, me],
                                            device_id=(dp, pc, pt), device_id_type=MESH)

    def got_copy(j, dc, dt):
        pc, pt, e = peer(dc, dt)
        return pltpu.make_async_remote_copy(zbuf.at[j, blk(e)], back.at[j, blk(e)], zsem.at[j, e], bsem.at[j, e],
                                            device_id=(dp, pc, pt), device_id_type=MESH)

    def w1_copies(s):
        slot = lax.rem(s, r1)
        cols = pl.ds(pl.multiple_of(s * f1, f1), f1)
        return (pltpu.make_async_copy(wg_hbm.at[:, cols], w1buf.at[slot, 0], w1sem.at[slot, 0]),
                pltpu.make_async_copy(wu_hbm.at[:, cols], w1buf.at[slot, 1], w1sem.at[slot, 1]))

    def w2_copy(s):
        slot = lax.rem(s, r2)
        cols = pl.ds(pl.multiple_of(s * f2, f2), f2)
        return pltpu.make_async_copy(wd_hbm.at[:, cols], w2buf.at[slot], w2sem.at[slot])

    def start_w1(s):
        for cp_ in w1_copies(s):
            cp_.start()

    def prefetch_w1():
        for s in range(r1):
            start_w1(jnp.int32(s))

    def prefetch_w2():
        for s in range(r2):
            w2_copy(jnp.int32(s)).start()

    prefetch_w1()
    prefetch_w2()

    barrier = pltpu.get_barrier_semaphore()
    for dc, dt in peers:
        pc, pt, _ = peer(dc, dt)
        pl.semaphore_signal(barrier, inc=1, device_id=(dp, pc, pt), device_id_type=MESH)
    pl.semaphore_wait(barrier, ne - 1)

    for j in range(nch):
        ri = lax.broadcasted_iota(jnp.int32, (rows, t), 0) + j * rows
        sel = jnp.where(ri == dr_ref[0:1, :], 1.0, 0.0) + jnp.where(ri == dr_ref[1:2, :], 1.0, 0.0)
        sel = sel.astype(BF)

        def pick(i, _):
            cols = pl.ds(pl.multiple_of(i * 512, 512), 512)
            send[j, :, cols] = dot(sel, h_ref[:, cols]).astype(BF)
            return 0

        lax.fori_loop(0, hd // 512, pick, 0)
        for dc, dt in peers:
            out_copy(j, dc, dt).start()
        recv[j, blk(me), :] = send[j, blk(me), :]

    for j in range(nch):
        for dc, dt in peers:
            in_copy(j, dc, dt).wait_recv()

        def up(s, _):
            slot = lax.rem(s, r1)
            for cp_ in w1_copies(s):
                cp_.wait()
            xx = recv[j]
            gg = dot(xx, w1buf[slot, 0])
            uu = dot(xx, w1buf[slot, 1])
            act[:, pl.ds(pl.multiple_of(s * f1, f1), f1)] = (gg * jax.nn.sigmoid(gg) * uu).astype(BF)

            @pl.when(s + r1 < n1)
            def _():
                start_w1(s + r1)
            return 0

        lax.fori_loop(0, n1, up, 0)
        if j + 1 < nch:
            prefetch_w1()

        def down(s, _):
            slot = lax.rem(s, r2)
            w2_copy(s).wait()
            zbuf[j, :, pl.ds(pl.multiple_of(s * f2, f2), f2)] = dot(act[...], w2buf[slot]).astype(BF)

            @pl.when(s + r2 < n2)
            def _():
                w2_copy(s + r2).start()
            return 0

        lax.fori_loop(0, n2, down, 0)
        if j + 1 < nch:
            prefetch_w2()
        for dc, dt in peers:
            home_copy(j, dc, dt).start()
        back[j, blk(me), :] = zbuf[j, blk(me), :]

    for j in range(nch):
        for dc, dt in peers:
            got_copy(j, dc, dt).wait_recv()

    ci = lax.broadcasted_iota(jnp.int32, (t, rows), 1)
    sel0 = [jnp.where(ci + j * rows == dc_ref[:, 0:1], 1.0, 0.0).astype(BF) for j in range(nch)]
    sel1 = [jnp.where(ci + j * rows == dc_ref[:, 1:2], 1.0, 0.0).astype(BF) for j in range(nch)]
    g0 = g_ref[:, 0:1]
    g1 = g_ref[:, 1:2]

    def combine(i, _):
        cols = pl.ds(pl.multiple_of(i * 512, 512), 512)
        z0 = sum(dot(sel0[j], back[j, :, cols]) for j in range(nch))
        z1 = sum(dot(sel1[j], back[j, :, cols]) for j in range(nch))
        y_ref[:, cols] = (h_ref[:, cols].astype(F32) + (g0 * z0 + g1 * z1)).astype(BF)
        return 0

    lax.fori_loop(0, hd // 512, combine, 0)

    for j in range(nch):
        for dc, dt in peers:
            out_copy(j, dc, dt).wait_send()
            home_copy(j, dc, dt).wait_send()


def moe(h, drow, dcol, gates, wg, wu, wd, *, ncp, ntp, nch, cid):
    t, hd = h.shape
    ff = wg.shape[1]
    ne = ncp * ntp
    rows = ne * CH
    f1, f2, r1, r2 = 256, 512, 2, 2
    vm = pl.BlockSpec(memory_space=pltpu.VMEM)
    hbm = pl.BlockSpec(memory_space=pl.ANY)
    dma = pltpu.SemaphoreType.DMA
    return pl.pallas_call(
        functools.partial(moe_kernel, ncp=ncp, ntp=ntp, nch=nch, f1=f1, f2=f2),
        in_specs=[vm, vm, vm, vm, hbm, hbm, hbm],
        out_specs=vm,
        out_shape=jax.ShapeDtypeStruct((t, hd), BF),
        scratch_shapes=[
            pltpu.VMEM((nch, rows, hd), BF), pltpu.VMEM((nch, rows, hd), BF),
            pltpu.VMEM((nch, rows, hd), BF), pltpu.VMEM((nch, rows, hd), BF),
            pltpu.VMEM((rows, ff), BF),
            pltpu.VMEM((r1, 2, hd, f1), BF), pltpu.VMEM((r2, ff, f2), BF),
            dma((nch, ne)), dma((nch, ne)), dma((nch, ne)), dma((nch, ne)),
            dma((r1, 2)), dma((r2,)),
        ],
        compiler_params=pltpu.CompilerParams(collective_id=cid, has_side_effects=True, vmem_limit_bytes=VMEM_LIMIT),
        name=f"moe{nch}",
        cost_estimate=pl.CostEstimate(flops=6 * nch * rows * hd * ff, bytes_accessed=6 * nch * hd * ff, transcendentals=0),
    )(h, drow, dcol, gates, wg, wu, wd)


def route(idx, ne):
    t = idx.shape[0]
    e = jnp.arange(ne, dtype=jnp.int32)[None, :]
    oh0 = (idx[:, 0:1] == e).astype(F32)
    oh1 = (idx[:, 1:2] == e).astype(F32)
    both = oh0 + oh1
    i = jnp.arange(t)
    before = dot((i[None, :] < i[:, None]).astype(F32), both)
    s0 = jnp.sum(before * oh0, axis=1).astype(jnp.int32)
    s1 = jnp.sum(before * oh1, axis=1).astype(jnp.int32)
    slot = jnp.stack([s0, s1], axis=1)
    code = (slot // CH) * (ne * CH) + idx * CH + slot % CH
    return code, jnp.max(jnp.sum(both, axis=0)).astype(jnp.int32)


def solution(mesh):
    ncp = mesh.shape["cp"]
    ntp = mesh.shape["tp"]
    ne = ncp * ntp
    rows_spec = P(("dp", "cp", "tp"), None)
    exp_spec = P(("cp", "tp"), None, None)

    def local(x, idx, gates, wq, wk, wv, wo, w1g, w1u, w2):
        code, most = route(idx, ne)
        most = lax.pmax(most, ("dp", "cp", "tp"))
        drow = jnp.pad(code.T, ((0, 6), (0, 0)))
        xs = lax.all_gather(x, "tp", axis=0, tiled=True)
        q = dot(xs, wq).astype(BF)
        kv = dot(xs, jnp.concatenate([wk, wv], axis=1)).astype(BF)
        kvs = lax.all_gather(kv, "cp", axis=0, tiled=True)
        o = flash(q, kvs[:, :HD], kvs[:, HD:], ncp)
        part = dot(o, wo)
        att = lax.psum_scatter(part, "tp", scatter_dimension=0, tiled=True)
        h = (x.astype(F32) + att).astype(BF)

        def few(args):
            return moe(*args, ncp=ncp, ntp=ntp, nch=2, cid=1)

        def many(args):
            return moe(*args, ncp=ncp, ntp=ntp, nch=4, cid=2)

        return lax.cond(most <= 2 * CH, few, many, (h, drow, code, gates, w1g[0], w1u[0], w2[0]))

    return jax.shard_map(local, mesh=mesh, in_specs=(rows_spec, rows_spec, rows_spec, P(None, "tp"), P(None, "tp"), P(None, "tp"), P("tp", None), exp_spec, exp_spec, exp_spec), out_specs=rows_spec, check_vma=False)
```

time: 1040 us -> 637 us (0.61)
  Pallas kernels: 0 us -> 381 us
  matrix products: 227 us -> 33.5 us
  waiting for transfers between devices: 344 us -> 152 us
  local copies, waits for them, and re-layouts: 182 us -> 8.7 us
  blocking collectives: 165 us -> 41.9 us
  other arithmetic: 91.2 us -> 4.32 us
    pallas_call x0 -> x2, Pallas kernels: none -> 381 us  [the longest x1 333 us: moe(): pl.pallas_call(functools.partial(moe_kernel, ncp=ncp, ntp=ntp, nch=nch, f...]
    dot_general x15 -> x4, matrix products: 227 us -> 33.5 us  [dot(): return jnp.dot(a, b, preferred_element_type=F32)]
    all_to_all x1 -> x0, blocking collectives: 165 us -> none  [local(): recv = lax.all_to_all(send, ('cp', 'tp'), 0, 0, tiled=True)]
    all_to_all x1 -> x0, waiting for transfers between devices: 157 us -> none  [local(): lax.all_to_all(z.reshape(ne, cap, hd), ('cp', 'tp'), 0, 0, tiled=True)]
    scatter x1 -> x0, local copies, waits for them, and re-layouts: 122 us -> none  [local(): send = jnp.zeros((ne, cap, hd), jnp.bfloat16).at[ea, slot].set(h[tok])]
    reduce_sum x3 -> x0, other arithmetic: 80.6 us -> none  [the longest x2 45.3 us: attention_residual(): l = l * c + jnp.sum(w, axis=-1)]
    pmax x0 -> x1, blocking collectives: none -> 41.9 us  [local(): most = lax.pmax(most, ('dp', 'cp', 'tp'))]
    reduce_scatter x1, waiting for transfers between devices: 103 us -> 66 us  [local(): att = lax.psum_scatter(part, 'tp', scatter_dimension=0, tiled=True)]
  transfers between devices with their start and end apart: 4 -> 3, of which waited for: 4 -> 3; matrix products, arithmetic and copies ran while one was open for 2% -> 2% of each run, Pallas kernels for 0% -> 0%
where the time goes in v1:
time: 637 us
  Pallas kernels  381 us (60%)
  waiting for transfers between devices  152 us (24%)
  blocking collectives  41.9 us (7%)
  matrix products  33.5 us (5%)
  between operations  14.5 us (2%)
  local copies, waits for them, and re-layouts  8.7 us (1%)
    pallas_call x1, Pallas kernels, moe(): pl.pallas_call(functools.partial(moe_kernel, ncp=ncp, ntp=ntp, nch=nch, f...  333 us
    reduce_scatter x1, waiting for transfers between devices, local(): att = lax.psum_scatter(part, 'tp', scatter_dimension=0, tiled=True)  66 us
    all_gather x1, waiting for transfers between devices, local(): xs = lax.all_gather(x, 'tp', axis=0, tiled=True)  55.6 us
    pallas_call x1, Pallas kernels, flash(): pl.pallas_call(kern, grid=(heads,), in_specs=[pl.BlockSpec((n, HD), lambd...  47.9 us
    pmax x1, blocking collectives, local(): most = lax.pmax(most, ('dp', 'cp', 'tp'))  41.9 us
    dot_general x4, matrix products, dot(): return jnp.dot(a, b, preferred_element_type=F32)  33.5 us
    all_gather x1, waiting for transfers between devices, local(): kvs = lax.all_gather(kv, 'cp', axis=0, tiled=True)  29.9 us
  transfers between devices with their start and end apart: 3, of which 3 were waited for; matrix products, arithmetic and copies ran while one was open for 2% of the time, Pallas kernels for 0%

profile of v1, /device:TPU:9, one launch (start us, length us, event | category | flops | bytes accessed | tf_op | source)
XLA Modules:
  0.0 636.5 jit_solution(1833598799865999719)
XLA Ops:
  6.5 0.0 all-gather.3.cloned.1.call-start
  6.5 0.7 all-gather.3.cloned.1.call-update
  7.3 0.0 all-gather.5.cloned.1.call-start
  7.3 55.6 %all-gather.3.cloned.1.call-done = bf16[1024,3584]{1,0:T(8,128)(2,1)} async-done(((bf16[256,3584]{1,0:T(8,128)(2,1)}), bf16[1024,3584]{1,0:T(8,128)(2,1)}) %all-gather.3.cloned.1.call-update) | async-done | bytes 7340048 | tf_op jit(solution)/shard_map/all_gather | solution.py:288
  62.9 6.4 %fusion.7 = bf16[1024,256]{1,0:T(8,128)(2,1)} fusion(bf16[1024,3584]{1,0:T(8,128)(2,1)} %all-gather.3.cloned.1.call-done, bf16[3584,128]{1,0:T(8,128)(2,1)} %param.17, bf16[3584,128]{1,0:T(8,128)(2,1)} %param.16), kind=kOutput, calls=%fused_computation.7 | convolution fusion | flops 1882980352 | bytes 9699328 | tf_op jit(solution)/shard_map/dot_general | solution.py:20
  69.4 0.0 all-gather.5.cloned.1.call-update
  69.4 0.0 reduce-scatter.2.cloned.1.call-start
  69.4 12.8 %convolution_convert_fusion.q_ref = bf16[1024,896]{1,0:T(8,128)(2,1)} fusion(bf16[1024,3584]{1,0:T(8,128)(2,1)} %all-gather.3.cloned.1.call-done, bf16[3584,896]{1,0:T(8,128)(2,1)} %param.15), kind=kOutput, calls=%fused_computation.5 | convolution fusion | flops 6577586176 | bytes 15597568 | tf_op jit(solution)/shard_map/dot_general | solution.py:20
  82.2 29.9 %all-gather.5.cloned.1.call-done = bf16[4096,256]{1,0:T(8,128)(2,1)} async-done(((bf16[1024,256]{1,0:T(8,128)(2,1)}), bf16[4096,256]{1,0:T(8,128)(2,1)}) %all-gather.5.cloned.1.call-update) | async-done | bytes 2097168 | tf_op jit(solution)/shard_map/all_gather | solution.py:291
  112.1 3.0 fusion.16
  115.1 47.9 %flash.1 = bf16[1024,896]{1,0:T(8,128)(2,1)} custom-call(bf16[1024,896]{1,0:T(8,128)(2,1)} %convolution_convert_fusion.q_ref, bf16[4096,128]{1,0:T(8,128)(2,1)} %get-tuple-element.113.k_ref, bf16[4096,128]{1,0:T(8,128)(2,1)} %get-tuple-element.112.v_ref), custom_call_target="tpu_custom_call" | custom-call | flops 7516192768 | bytes 3670016 | tf_op jit(solution)/shard_map/flash/pallas_call | solution.py:65
  163.0 14.1 %fusion.18 = f32[1024,3584]{1,0:T(8,128)} fusion(bf16[1024,896]{1,0:T(8,128)(2,1)} %flash.1, bf16[896,3584]{1,0:T(8,128)(2,1)} %param.18), kind=kOutput, calls=%fused_computation.28 | convolution fusion | flops 6576668672 | bytes 22937600 | tf_op jit(solution)/shard_map/dot_general | solution.py:20
  177.1 0.0 copy-start.1
  177.1 0.0 copy-start
  177.1 0.0 reduce-scatter.2.cloned.1.call-update
  177.1 0.7 copy-done.1
  177.8 0.2 select_reduce_fusion.1
  178.0 0.6 reduce_max.9
  179.3 41.9 %pmax.7 = s32[]{:T(128)} all-reduce(s32[]{:T(128)S(6)} %convert_element_type.56), channel_id=1, replica_groups=mesh['dp'=2,'cp'=4,'tp'=4] {'dp','cp','tp'}, use_global_device_ids=true, to_apply=%region_2.3 | all-reduce | flops 1 | bytes 8 | tf_op jit(solution)/shard_map/pmax | solution.py:286
  221.8 0.0 copy-start.2
  221.9 66.0 %reduce-scatter.2.cloned.1.call-done = f32[256,3584]{1,0:T(8,128)} async-done(((f32[1024,3584]{1,0:T(8,128)}), f32[256,3584]{1,0:T(8,128)}) %reduce-scatter.2.cloned.1.call-update) | async-done | bytes 3670032 | tf_op jit(solution)/shard_map/reduce_scatter | solution.py:294
  287.9 0.0 copy-done
  287.9 3.7 add_convert_fusion
  291.6 0.0 copy-done.2
  291.6 335.5 %conditional.1 = (bf16[256,3584]{1,0:T(8,128)(2,1)}) conditional(s32[]{:T(128)} %convert_element_type.57, (bf16[256,3584]{1,0:T(8,128)(2,1)}, s32[2,256]{1,0:T(2,128)S(1)}, s32[256,2]{0,1:T(2,128)S(1)}, f32[256,2]{0,1:T(2,128)S(1)}, bf16[1,3584,2560]{2,1,0:T(8,128)(2,1)}, /*index=5*/bf16[1,3584,2560]{2,1,0:T(8,128)(2,1)}, ...), branch_computations={%region_6.7_spmd, %region_7.8_spmd} | conditional | flops 56371445760 | bytes 220219392 | solution.py:303
  291.6 0.6 pad.5.dr_ref
  292.2 0.8 copy.31.dc_ref
  293.0 0.8 copy.32.g_ref
  293.8 333.1 %moe4.1 = bf16[256,3584]{1,0:T(8,128)(2,1)} custom-call(bf16[256,3584]{1,0:T(8,128)(2,1)} %get-tuple-element.36.h_ref, s32[8,256]{1,0:T(8,128)} %pad.5.dr_ref, s32[256,2]{1,0:T(8,128)} %copy.31.dc_ref, f32[256,2]{1,0:T(8,128)} %copy.32.g_ref, bf16[3584,2560]{1,0:T(8,128)(2,1)} %bitcast.25, bf16[3584,2560]{1,0:T(8,128)(2,1)} %bitcast.27, ...), custom_call_target="tpu_custom_call" | custom-call | flops 56371445760 | bytes 220200960 | tf_op jit(solution)/shard_map/cond/branch_0_fun/moe4/pallas_call | solution.py:243
  627.1 2.8 copy.39
  (5 shorter events, 0.1 us)
Async XLA Ops:
  6.5 56.4 %all-gather.3.cloned.1.call-start = ((), (), s32[]{:S(2)}) async-start(), calls=%async_computation.1 | async-start | bytes 9175040 | tf_op jit(solution)/shard_map/all_gather | solution.py:288
  7.3 104.8 %all-gather.5.cloned.1.call-start = ((), (), s32[]{:S(2)}) async-start(), calls=%async_computation.2 | async-start | bytes 2621440 | tf_op jit(solution)/shard_map/all_gather | solution.py:291
  69.4 218.5 %reduce-scatter.2.cloned.1.call-start = ((), (), s32[]{:S(2)}) async-start(), calls=%async_computation.3 | async-start | bytes 18350080 | tf_op jit(solution)/shard_map/reduce_scatter | solution.py:294
  177.1 0.7 copy-start.1
  177.1 110.8 %copy-start = (bf16[256,3584]{1,0:T(8,128)(2,1)S(1)}, bf16[256,3584]{1,0:T(8,128)(2,1)}, u32[]{:S(2)}) copy-start(bf16[256,3584]{1,0:T(8,128)(2,1)} %param.12) | copy-start | bytes 5505028
  221.8 69.7 %copy-start.2 = (f32[256,2]{0,1:T(2,128)S(1)}, f32[256,2]{0,1:T(2,128)}, u32[]{:S(2)}) copy-start(f32[256,2]{0,1:T(2,128)} %param.14) | copy-start | bytes 6148
Sparse Core Ops, SparseCore 0:
  8.9 54.0 all-gather.2
  69.5 42.5 all-gather.4
  177.3 110.5 reduce-scatter.1

commit v2 on v1

--- a/solution.py
+++ b/solution.py
@@ -20,23 +20,190 @@
     return jnp.dot(a, b, preferred_element_type=F32)
 
 
-def flash_kernel(q_ref, k_ref, v_ref, o_ref, vt_ref, *, seg, ncp, scale):
+def att_kernel(x_hbm, wq_hbm, wk_hbm, wv_hbm, wo_hbm, most_ref, h_ref, mx_ref,
+               xs, wq, wkv, wo_a, wo_b, q_a, q_b, kb, vt, o_a, o_s, o_b, part, pin, cnt,
+               lsem, cx_s, cx_r, yx_s, yx_r, fx_s, fx_r, kv_s, kv_r, wy_s, wy_r, wx_s, wx_r,
+               wu_s, wu_r, wd_s, wd_r, o_ss, o_rs, p_ss, p_rs, n_s, n_r, *, nd, ncp, ntp, scale):
+    d = lax.axis_index("dp")
     c = lax.axis_index("cp")
+    t = lax.axis_index("tp")
+    y = t // 2
+    k = lax.rem(t, 2)
+    t_c = 2 * y + 1 - k
+    t_y = 2 * (1 - y) + k
+    t_z = 2 * (1 - y) + 1 - k
+    rb = xs.shape[1]
+    hd = xs.shape[2]
+    seg = 2 * rb
+    hk = rb // 2
+    heads = q_a.shape[1] // HD
+    pr = wo_a.shape[0] // (nd * ncp)
     last = 2 * ncp - 1
-
-    @pl.when(pl.program_id(0) == 0)
-    def _():
-        for b in range(2 * ncp):
-            vt_ref[:, b * seg:(b + 1) * seg] = v_ref[b * seg:(b + 1) * seg, :].T
-
-    def place(g):
-        r = jnp.minimum(g, last - g)
-        return pl.multiple_of((2 * r + jnp.where(g == r, 0, 1)) * seg, seg)
+    mine = jnp.where(y == 0, c, last - c)
+    other = last - mine
+    me = (d * ncp + c) * ntp + t
+
+    def rcopy(src, dst, ss, rs, dd, cc, tt):
+        return pltpu.make_async_remote_copy(src, dst, ss, rs, device_id=(dd, cc, tt), device_id_type=MESH)
+
+    loads = [
+        pltpu.make_async_copy(wk_hbm, wkv.at[:, 0:HD], lsem.at[0]),
+        pltpu.make_async_copy(wv_hbm, wkv.at[:, HD:2 * HD], lsem.at[1]),
+        pltpu.make_async_copy(x_hbm, xs.at[t], lsem.at[2]),
+        pltpu.make_async_copy(wq_hbm, wq, lsem.at[3]),
+        pltpu.make_async_copy(wo_hbm, wo_a, lsem.at[4]),
+    ]
+    for cp_ in loads:
+        cp_.start()
+
+    n_all = nd * ncp * ntp
+    others = [(a, b, e) for a in range(nd) for b in range(ncp) for e in range(ntp) if (a, b, e) != (0, 0, 0)]
+
+    def rel(a, b, e):
+        return lax.rem(d + a, nd), lax.rem(c + b, ncp), lax.rem(t + e, ntp)
+
+    barrier = pltpu.get_barrier_semaphore()
+    for o in others:
+        pl.semaphore_signal(barrier, inc=1, device_id=rel(*o), device_id_type=MESH)
+    pl.semaphore_wait(barrier, n_all - 1)
+
+    def piece(dd, cc):
+        return pl.ds(pl.multiple_of((dd * ncp + cc) * pr, pr), pr)
+
+    def half(i):
+        return pl.ds(i * hk, hk)
+
+    wy = rcopy(wo_hbm.at[piece(d, c)], wo_b.at[piece(d, c)], wy_s, wy_r, d, c, t_y)
+    wy.start()
+    yx = [rcopy(x_hbm.at[half(i)], xs.at[t, half(i)], yx_s.at[i], yx_r.at[i], d, c, t_y) for i in range(2)]
+    yx_in = [rcopy(x_hbm.at[half(i)], xs.at[t_y, half(i)], yx_s.at[i], yx_r.at[i], d, c, t_y) for i in range(2)]
+    for cp_ in yx:
+        cp_.start()
+    cx = rcopy(x_hbm, xs.at[t], cx_s, cx_r, d, c, t_c)
+    cx_in = rcopy(x_hbm, xs.at[t_c], cx_s, cx_r, d, c, t_c)
+    cx.start()
+    cnt[me] = most_ref[...]
+    for i, o in enumerate(others):
+        dd, cc, tt = rel(*o)
+        rcopy(most_ref, cnt.at[me], n_s.at[i], n_r.at[me], dd, cc, tt).start()
+
+    zpeers = list(range(1, ncp))
+
+    def kv_copies(g, at, n, i, dc, here):
+        cc = lax.rem(c + dc, ncp)
+        src = c if here else cc
+        rows = pl.ds(at, n)
+        return (rcopy(kb.at[g, rows], kb.at[g, rows], kv_s.at[cc, 2 * i], kv_r.at[src, 2 * i], d, cc, t),
+                rcopy(vt.at[g, :, rows], vt.at[g, :, rows], kv_s.at[cc, 2 * i + 1], kv_r.at[src, 2 * i + 1], d, cc, t))
+
+    def kv_rows(g, at, n, src):
+        r = dot(src, wkv[...])
+        kb[g, pl.ds(at, n), :] = r[:, :HD].astype(BF)
+        vt[g, :, pl.ds(at, n)] = r[:, HD:].astype(BF).T
+
+    def kv_send(g, at, n, i):
+        for dc in zpeers:
+            for cp_ in kv_copies(g, at, n, i, dc, True):
+                cp_.start()
+
+    at_k = pl.multiple_of(k * rb, rb)
+    at_c = pl.multiple_of((1 - k) * rb, rb)
+
+    for i in (0, 1, 2):
+        loads[i].wait()
+    kv_rows(mine, at_k, rb, xs[t])
+    kv_send(mine, at_k, rb, 0)
+    cx_in.wait_recv()
+    kv_rows(mine, at_c, rb, xs[t_c])
+    kv_send(mine, at_c, rb, 1)
+    loads[3].wait()
+
+    def q_rows(q_ref, at, src):
+        for lo in range(0, heads * HD, 256):
+            hi = min(lo + 256, heads * HD)
+            q_ref[pl.ds(at, rb), lo:hi] = dot(src, wq[:, lo:hi]).astype(BF)
+
+    q_rows(q_a, at_k, xs[t])
+    q_rows(q_a, at_c, xs[t_c])
+
+    def x_copy(cc, there):
+        dd = 1 - d if there else d
+        return rcopy(wo_b.at[piece(dd, cc)], wo_b.at[piece(dd, cc)], wx_s.at[cc], wx_r.at[cc], 1 - d, c, t)
+
+    def up_copy(cc, to):
+        return rcopy(wo_b.at[piece(d, cc)], wo_b.at[piece(d, cc)], wu_s.at[cc], wu_r.at[cc], d, to, t)
+
+    def dn_copy(cc, to):
+        return rcopy(wo_b.at[piece(d, cc)], wo_b.at[piece(d, cc)], wd_s.at[cc], wd_r.at[cc], d, to, t)
+
+    c_up = jnp.minimum(c + 1, ncp - 1)
+    c_dn = jnp.maximum(c - 1, 0)
+
+    def wo_first():
+        rcopy(wo_hbm.at[piece(d, c)], wo_b.at[piece(d, c)], wy_s, wy_r, d, c, t_y).wait_recv()
+        x_copy(c, False).start()
+
+        @pl.when(c < ncp - 1)
+        def _():
+            up_copy(c, c_up).start()
+
+        @pl.when(c > 0)
+        def _():
+            dn_copy(c, c_dn).start()
+
+    def wo_next(i):
+        below = jnp.maximum(c - i, 0)
+        above = jnp.minimum(c + i, ncp - 1)
+
+        @pl.when(c - i >= 0)
+        def _():
+            up_copy(below, c_dn).wait_recv()
+
+            @pl.when(c < ncp - 1)
+            def _():
+                up_copy(below, c_up).start()
+            x_copy(below, False).start()
+
+        @pl.when(c + i <= ncp - 1)
+        def _():
+            dn_copy(above, c_up).wait_recv()
+
+            @pl.when(c > 0)
+            def _():
+                dn_copy(above, c_dn).start()
+            x_copy(above, False).start()
+
+    wo_first()
+
+    for i in range(2):
+        yx_in[i].wait_recv()
+        fwd = rcopy(xs.at[t_y, half(i)], xs.at[t_y, half(i)], fx_s.at[i], fx_r.at[i], d, c, t_c)
+        fwd.start()
+        a0 = pl.multiple_of(at_k + i * hk, hk)
+        kv_rows(other, a0, hk, xs[t_y, i * hk:(i + 1) * hk])
+        kv_send(other, a0, hk, 2 + i)
+        rcopy(xs.at[t_z, half(i)], xs.at[t_z, half(i)], fx_s.at[i], fx_r.at[i], d, c, t_c).wait_recv()
+        a1 = pl.multiple_of(at_c + i * hk, hk)
+        kv_rows(other, a1, hk, xs[t_z, i * hk:(i + 1) * hk])
+        kv_send(other, a1, hk, 4 + i)
+        if i == 0:
+            wo_next(1)
+    q_rows(q_b, at_k, xs[t_y])
+    q_rows(q_b, at_c, xs[t_z])
+
+    for dc in zpeers:
+        cc = lax.rem(c + dc, ncp)
+        gm = jnp.where(y == 0, cc, last - cc)
+        go = last - gm
+        for i, (g, at, n) in enumerate([(gm, at_k, rb), (gm, at_c, rb),
+                                        (go, at_k, hk), (go, pl.multiple_of(at_k + hk, hk), hk),
+                                        (go, at_c, hk), (go, pl.multiple_of(at_c + hk, hk), hk)]):
+            for cp_ in kv_copies(g, at, n, i, dc, False):
+                cp_.wait_recv()
 
     def step(g, carry, qb, masked):
         m, l, acc = carry
-        at = place(g)
-        s = lax.dot_general(k_ref[pl.ds(at, seg), :], qb, (((1,), (1,)), ((), ())), preferred_element_type=F32) * scale
+        s = lax.dot_general(kb[g], qb, (((1,), (1,)), ((), ())), preferred_element_type=F32) * scale
         if masked:
             ki = lax.broadcasted_iota(jnp.int32, s.shape, 0)
             qi = lax.broadcasted_iota(jnp.int32, s.shape, 1)
@@ -45,34 +212,132 @@
         w = jnp.exp(s - mn)
         a = jnp.exp(m - mn)
         l = l * a + jnp.sum(w, axis=0, keepdims=True)
-        acc = acc * a + dot(vt_ref[:, pl.ds(at, seg)], w.astype(BF))
+        acc = acc * a + dot(vt[g], w.astype(BF))
         return mn, l, acc
 
-    for half in range(2):
-        mine = c if half == 0 else last - c
-        qb = q_ref[half * seg:(half + 1) * seg, :]
+    def attend(q_ref, hcols, count):
+        qb = q_ref[:, hcols]
         carry = (jnp.full((1, seg), NEG, F32), jnp.zeros((1, seg), F32), jnp.zeros((HD, seg), F32))
-        carry = lax.fori_loop(0, mine, lambda g, cr: step(g, cr, qb, False), carry)
-        m, l, acc = step(mine, carry, qb, True)
-        o_ref[half * seg:(half + 1) * seg, :] = (acc / l).T.astype(BF)
-
-
-def flash(q, k, v, ncp):
-    n, d = q.shape
-    heads = d // HD
-    kern = functools.partial(flash_kernel, seg=n // 2, ncp=ncp, scale=HD ** -0.5)
-    full = pl.BlockSpec(k.shape, lambda h: (0, 0))
+        carry = lax.fori_loop(0, count, lambda g, cr: step(g, cr, qb, False), carry)
+        m, l, acc = step(count, carry, qb, True)
+        return (acc / l).T.astype(BF)
+
+    def o_copy(j):
+        cols = pl.ds(pl.multiple_of(j * HD, HD), HD)
+        return rcopy(o_s.at[:, cols], o_b.at[:, cols], o_ss.at[j], o_rs.at[j], d, c, t_y)
+
+    def head(j, _):
+        hcols = pl.ds(pl.multiple_of(j * HD, HD), HD)
+        o_s[:, hcols] = attend(q_b, hcols, other)
+        o_copy(j).start()
+        o_a[:, hcols] = attend(q_a, hcols, mine)
+        return 0
+
+    lax.fori_loop(0, 1, head, 0)
+    wo_next(2)
+    lax.fori_loop(1, 4, head, 0)
+    wo_next(3)
+    lax.fori_loop(4, heads, head, 0)
+
+    for cc in range(ncp):
+        x_copy(cc, True).wait_recv()
+    loads[4].wait()
+    for j in range(heads):
+        o_copy(j).wait_recv()
+
+    nc = hd // 512
+
+    def p_copy(i):
+        cols = pl.ds(pl.multiple_of(i * 512, 512), 512)
+        return rcopy(part.at[:, cols], pin.at[:, cols], p_ss.at[i], p_rs.at[i], d, c, t_c)
+
+    def proj(at, cols):
+        rows = pl.ds(at, rb)
+        return dot(o_a[rows, :], wo_a[:, cols]) + dot(o_b[rows, :], wo_b[:, cols])
+
+    def give(i, _):
+        cols = pl.ds(pl.multiple_of(i * 512, 512), 512)
+        part[:, cols] = proj(at_c, cols)
+        p_copy(i).start()
+        return 0
+
+    lax.fori_loop(0, nc, give, 0)
+
+    def keep(i, _):
+        cols = pl.ds(pl.multiple_of(i * 512, 512), 512)
+        own = proj(at_k, cols)
+        p_copy(i).wait_recv()
+        h_ref[:, cols] = (xs[t, :, cols].astype(F32) + (own + pin[:, cols])).astype(BF)
+        return 0
+
+    lax.fori_loop(0, nc, keep, 0)
+
+    for o in others:
+        dd, cc, tt = rel(*o)
+        src = (dd * ncp + cc) * ntp + tt
+        rcopy(most_ref, cnt.at[src], n_s.at[0], n_r.at[src], dd, cc, tt).wait_recv()
+    mx_ref[...] = jnp.max(cnt[...], axis=0)
+
+    wy.wait_send()
+    cx.wait_send()
+    for i in range(2):
+        yx[i].wait_send()
+        rcopy(xs.at[t_y, half(i)], xs.at[t_y, half(i)], fx_s.at[i], fx_r.at[i], d, c, t_c).wait_send()
+    for i, o in enumerate(others):
+        dd, cc, tt = rel(*o)
+        rcopy(most_ref, cnt.at[me], n_s.at[i], n_r.at[me], dd, cc, tt).wait_send()
+    for dc in zpeers:
+        for i, (g, at, n) in enumerate([(mine, at_k, rb), (mine, at_c, rb),
+                                        (other, at_k, hk), (other, pl.multiple_of(at_k + hk, hk), hk),
+                                        (other, at_c, hk), (other, pl.multiple_of(at_c + hk, hk), hk)]):
+            for cp_ in kv_copies(g, at, n, i, dc, True):
+                cp_.wait_send()
+    for cc in range(ncp):
+        x_copy(cc, False).wait_send()
+
+        @pl.when((cc <= c) & (c < ncp - 1))
+        def _():
+            up_copy(cc, c_up).wait_send()
+
+        @pl.when((cc >= c) & (c > 0))
+        def _():
+            dn_copy(cc, c_dn).wait_send()
+    for j in range(heads):
+        o_copy(j).wait_send()
+    for i in range(nc):
+        p_copy(i).wait_send()
+
+
+def attention(x, wq, wk, wv, wo, most, *, nd, ncp, ntp, cid):
+    rb, hd = x.shape
+    ql = wq.shape[1]
+    seg = 2 * rb
+    heads = ql // HD
+    nseg = 2 * ncp
+    n_all = nd * ncp * ntp
+    hbm = pl.BlockSpec(memory_space=pl.ANY)
+    vm = pl.BlockSpec(memory_space=pltpu.VMEM)
+    dma = pltpu.SemaphoreType.DMA
+    V = pltpu.VMEM
     return pl.pallas_call(
-        kern,
-        grid=(heads,),
-        in_specs=[pl.BlockSpec((n, HD), lambda h: (0, h)), full, full],
-        out_specs=pl.BlockSpec((n, HD), lambda h: (0, h)),
-        out_shape=jax.ShapeDtypeStruct((n, d), BF),
-        scratch_shapes=[pltpu.VMEM((HD, k.shape[0]), BF)],
-        compiler_params=pltpu.CompilerParams(vmem_limit_bytes=VMEM_LIMIT, dimension_semantics=("arbitrary",)),
-        name="flash",
-        cost_estimate=pl.CostEstimate(flops=heads * n * k.shape[0] * HD * 2, bytes_accessed=4 * n * d, transcendentals=heads * n * k.shape[0] // 2),
-    )(q, k, v)
+        functools.partial(att_kernel, nd=nd, ncp=ncp, ntp=ntp, scale=HD ** -0.5),
+        in_specs=[hbm, hbm, hbm, hbm, hbm, vm],
+        out_specs=[vm, vm],
+        out_shape=[jax.ShapeDtypeStruct((rb, hd), BF), jax.ShapeDtypeStruct(most.shape, most.dtype)],
+        scratch_shapes=[
+            V((ntp, rb, hd), BF), V((hd, ql), BF), V((hd, 2 * HD), BF), V((ql, hd), BF), V((ql, hd), BF),
+            V((seg, ql), BF), V((seg, ql), BF), V((nseg, seg, HD), BF), V((nseg, HD, seg), BF),
+            V((seg, ql), BF), V((seg, ql), BF), V((seg, ql), BF), V((rb, hd), F32), V((rb, hd), F32),
+            V((n_all,) + most.shape, most.dtype),
+            dma((5,)), dma(()), dma(()), dma((2,)), dma((2,)), dma((2,)), dma((2,)),
+            dma((ncp, 12)), dma((ncp, 12)), dma(()), dma(()), dma((ncp,)), dma((ncp,)),
+            dma((ncp,)), dma((ncp,)), dma((ncp,)), dma((ncp,)), dma((heads,)), dma((heads,)),
+            dma((hd // 512,)), dma((hd // 512,)), dma((n_all - 1,)), dma((n_all,)),
+        ],
+        compiler_params=pltpu.CompilerParams(collective_id=cid, has_side_effects=True, vmem_limit_bytes=VMEM_LIMIT),
+        name="att",
+        cost_estimate=pl.CostEstimate(flops=60_000_000_000, bytes_accessed=30_000_000, transcendentals=0),
+    )(x, wq, wk, wv, wo, most)
 
 
 def moe_kernel(h_ref, dr_ref, dc_ref, g_ref, wg_hbm, wu_hbm, wd_hbm, y_ref,
@@ -283,16 +548,8 @@
 
     def local(x, idx, gates, wq, wk, wv, wo, w1g, w1u, w2):
         code, most = route(idx, ne)
-        most = lax.pmax(most, ("dp", "cp", "tp"))
         drow = jnp.pad(code.T, ((0, 6), (0, 0)))
-        xs = lax.all_gather(x, "tp", axis=0, tiled=True)
-        q = dot(xs, wq).astype(BF)
-        kv = dot(xs, jnp.concatenate([wk, wv], axis=1)).astype(BF)
-        kvs = lax.all_gather(kv, "cp", axis=0, tiled=True)
-        o = flash(q, kvs[:, :HD], kvs[:, HD:], ncp)
-        part = dot(o, wo)
-        att = lax.psum_scatter(part, "tp", scatter_dimension=0, tiled=True)
-        h = (x.astype(F32) + att).astype(BF)
+        h, most = attention(x, wq, wk, wv, wo, jnp.full((8, 128), most), nd=mesh.shape["dp"], ncp=ncp, ntp=ntp, cid=3)
 
         def few(args):
             return moe(*args, ncp=ncp, ntp=ntp, nch=2, cid=1)
@@ -300,6 +557,6 @@
         def many(args):
             return moe(*args, ncp=ncp, ntp=ntp, nch=4, cid=2)
 
-        return lax.cond(most <= 2 * CH, few, many, (h, drow, code, gates, w1g[0], w1u[0], w2[0]))
+        return lax.cond(most[0, 0] <= 2 * CH, few, many, (h, drow, code, gates, w1g[0], w1u[0], w2[0]))
 
     return jax.shard_map(local, mesh=mesh, in_specs=(rows_spec, rows_spec, rows_spec, P(None, "tp"), P(None, "tp"), P(None, "tp"), P("tp", None), exp_spec, exp_spec, exp_spec), out_specs=rows_spec, check_vma=False)

time: 637 us -> 496 us (0.78)
  waiting for transfers between devices: 152 us -> 0 us
  Pallas kernels: 381 us -> 484 us
  blocking collectives: 41.9 us -> 0 us
  matrix products: 33.5 us -> 0.2 us
  between operations: 14.5 us -> 1.36 us
    pallas_call x1, Pallas kernels: 47.9 us -> 147 us  [attention(): pl.pallas_call(functools.partial(att_kernel, nd=nd, ncp=ncp, ntp=ntp, sca...]
    all_gather x2 -> x0, waiting for transfers between devices: 85.5 us -> none  [the longest x1 55.6 us: local(): xs = lax.all_gather(x, 'tp', axis=0, tiled=True)]
    reduce_scatter x1 -> x0, waiting for transfers between devices: 66 us -> none  [local(): att = lax.psum_scatter(part, 'tp', scatter_dimension=0, tiled=True)]
    pmax x1 -> x0, blocking collectives: 41.9 us -> none  [local(): most = lax.pmax(most, ('dp', 'cp', 'tp'))]
    dot_general x4 -> x1, matrix products: 33.5 us -> 0.2 us  [dot(): return jnp.dot(a, b, preferred_element_type=F32)]
  transfers between devices with their start and end apart: 3 -> 0, of which waited for: 3 -> 0; matrix products, arithmetic and copies ran while one was open for 2% -> 0% of each run, Pallas kernels for 0% -> 0%
where the time goes in v2:
time: 496 us
  Pallas kernels  484 us (98%)
  local copies, waits for them, and re-layouts  7.58 us (2%)
    pallas_call x1, Pallas kernels, moe(): pl.pallas_call(functools.partial(moe_kernel, ncp=ncp, ntp=ntp, nch=nch, f...  337 us
    pallas_call x1, Pallas kernels, attention(): pl.pallas_call(functools.partial(att_kernel, nd=nd, ncp=ncp, ntp=ntp, sca...  147 us

profile of v2, /device:TPU:9, one launch (start us, length us, event | category | flops | bytes accessed | tf_op | source)
XLA Modules:
  0.0 495.8 jit_solution(7474200839139411564)
XLA Ops:
  0.0 0.8 fusion.5
  0.8 0.2 select_reduce_fusion.1
  1.0 0.6 reduce_max.9
  2.2 0.7 fusion.6
  2.9 0.7 fusion.4
  3.7 0.6 broadcast_in_dim.2.most_ref
  4.3 0.0 copy-start
  4.3 147.4 %att.1 = (bf16[256,3584]{1,0:T(8,128)(2,1)}, s32[8,128]{1,0:T(8,128)}) custom-call(bf16[256,3584]{1,0:T(8,128)(2,1)} %x_hbm.1, bf16[3584,896]{1,0:T(8,128)(2,1)} %wq_hbm.1, bf16[3584,128]{1,0:T(8,128)(2,1)} %wk_hbm.1, bf16[3584,128]{1,0:T(8,128)(2,1)} %wv_hbm.1, bf16[896,3584]{1,0:T(8,128)(2,1)} %wo_hbm.1, s32[8,128]{1,0:T(8,128)} %broadcast_in_dim.2.most_ref), custom_call_target="tpu_custom_call" | custom-call | flops 60000002048 | bytes 30000000 | tf_op jit(solution)/shard_map/att/pallas_call | solution.py:322
  151.7 1.2 slice.11
  153.5 0.0 copy-done
  153.5 339.4 %conditional.1 = (bf16[256,3584]{1,0:T(8,128)(2,1)}) conditional(s32[]{:T(128)} %bitcast.8, (bf16[256,3584]{1,0:T(8,128)(2,1)}, s32[2,256]{1,0:T(2,128)S(1)}, s32[256,2]{0,1:T(2,128)S(1)}, f32[256,2]{0,1:T(2,128)S(1)}, bf16[1,3584,2560]{2,1,0:T(8,128)(2,1)}, /*index=5*/bf16[1,3584,2560]{2,1,0:T(8,128)(2,1)}, bf16[1,2560,3584]{2,1,0:T(8,128)(2,1)}, ...), branch_computations={%region_4.5_spmd, %region_5.6_spmd} | conditional | flops 56371445760 | bytes 220219392 | solution.py:560
  153.8 0.6 pad.5.dr_ref
  154.4 0.8 copy.30.g_ref
  155.1 0.8 copy.29.dc_ref
  155.9 336.7 %moe4.1 = bf16[256,3584]{1,0:T(8,128)(2,1)} custom-call(bf16[256,3584]{1,0:T(8,128)(2,1)} %get-tuple-element.36.h_ref, s32[8,256]{1,0:T(8,128)} %pad.5.dr_ref, s32[256,2]{1,0:T(8,128)} %copy.29.dc_ref, f32[256,2]{1,0:T(8,128)} %copy.30.g_ref, bf16[3584,2560]{1,0:T(8,128)(2,1)} %bitcast.19, bf16[3584,2560]{1,0:T(8,128)(2,1)} %bitcast.21, ...), custom_call_target="tpu_custom_call" | custom-call | flops 56371445760 | bytes 220200960 | tf_op jit(solution)/shard_map/cond/branch_0_fun/moe4/pallas_call | solution.py:508
  492.9 2.8 copy.36
  (2 shorter events, 0.0 us)
Async XLA Ops:
  4.3 149.3 %copy-start = (f32[256,2]{0,1:T(2,128)S(1)}, f32[256,2]{0,1:T(2,128)}, u32[]{:S(2)}) copy-start(f32[256,2]{0,1:T(2,128)} %param.14) | copy-start | bytes 6148

commit v3 on v2

--- a/solution.py
+++ b/solution.py
@@ -14,16 +14,19 @@
 MESH = pl.DeviceIdType.MESH
 VMEM_LIMIT = 67_000_000
 CH = 16
+NCH = 2
 
 
 def dot(a, b):
     return jnp.dot(a, b, preferred_element_type=F32)
 
 
-def att_kernel(x_hbm, wq_hbm, wk_hbm, wv_hbm, wo_hbm, most_ref, h_ref, mx_ref,
-               xs, wq, wkv, wo_a, wo_b, q_a, q_b, kb, vt, o_a, o_s, o_b, part, pin, cnt,
+def layer_kernel(x_hbm, wq_hbm, wk_hbm, wv_hbm, wo_hbm, idx_ref, g_ref, wg_hbm, wu_hbm, wd_hbm,
+                 y_ref, h_ref, code_ref, mx_ref,
+               xs, wq, wkv, wo_a, wo_b, qq, kb, vt, oo, o_b, part, pin, cnt, top, s0, s1, bias, acc,
+               send, recv, act, w2buf,
                lsem, cx_s, cx_r, yx_s, yx_r, fx_s, fx_r, kv_s, kv_r, wy_s, wy_r, wx_s, wx_r,
-               wu_s, wu_r, wd_s, wd_r, o_ss, o_rs, p_ss, p_rs, n_s, n_r, *, nd, ncp, ntp, scale):
+               wu_s, wu_r, wd_s, wd_r, wf_s, wf_r, o_ss, o_rs, p_ss, p_rs, n_s, n_r, ssem, rsem, zsem, bsem, w1sem, w2sem, *, nd, ncp, ntp, scale):
     d = lax.axis_index("dp")
     c = lax.axis_index("cp")
     t = lax.axis_index("tp")
@@ -36,7 +39,8 @@
     hd = xs.shape[2]
     seg = 2 * rb
     hk = rb // 2
-    heads = q_a.shape[1] // HD
+    heads = qq.shape[2] // HD
+    q_a, q_b, o_a, o_s = qq.at[0], qq.at[1], oo.at[0], oo.at[1]
     pr = wo_a.shape[0] // (nd * ncp)
     last = 2 * ncp - 1
     mine = jnp.where(y == 0, c, last - c)
@@ -50,7 +54,7 @@
         pltpu.make_async_copy(wk_hbm, wkv.at[:, 0:HD], lsem.at[0]),
         pltpu.make_async_copy(wv_hbm, wkv.at[:, HD:2 * HD], lsem.at[1]),
         pltpu.make_async_copy(x_hbm, xs.at[t], lsem.at[2]),
-        pltpu.make_async_copy(wq_hbm, wq, lsem.at[3]),
+        pltpu.make_async_copy(wq_hbm, wq.at[:, 0:wq_hbm.shape[1]], lsem.at[3]),
         pltpu.make_async_copy(wo_hbm, wo_a, lsem.at[4]),
     ]
     for cp_ in loads:
@@ -74,18 +78,39 @@
         return pl.ds(i * hk, hk)
 
     wy = rcopy(wo_hbm.at[piece(d, c)], wo_b.at[piece(d, c)], wy_s, wy_r, d, c, t_y)
-    wy.start()
     yx = [rcopy(x_hbm.at[half(i)], xs.at[t, half(i)], yx_s.at[i], yx_r.at[i], d, c, t_y) for i in range(2)]
     yx_in = [rcopy(x_hbm.at[half(i)], xs.at[t_y, half(i)], yx_s.at[i], yx_r.at[i], d, c, t_y) for i in range(2)]
+    far = jnp.where(c < ncp // 2, ncp - 1, 0)
+    wf = rcopy(wo_hbm.at[piece(d, far)], wo_b.at[piece(d, far)], wf_s, wf_r, d, c, t_y)
+
+    wy.start()
     for cp_ in yx:
         cp_.start()
+    wf.start()
     cx = rcopy(x_hbm, xs.at[t], cx_s, cx_r, d, c, t_c)
     cx_in = rcopy(x_hbm, xs.at[t_c], cx_s, cx_r, d, c, t_c)
     cx.start()
-    cnt[me] = most_ref[...]
+
+    ne = ncp * ntp
+    lane = lax.broadcasted_iota(jnp.int32, (rb, 128), 1)
+    e0, e1 = idx_ref[:, 0:1], idx_ref[:, 1:2]
+    oh0 = jnp.where(lane == e0, 1.0, 0.0)
+    oh1 = jnp.where(lane == e1, 1.0, 0.0)
+    both = oh0 + oh1
+    tri = jnp.where(lax.broadcasted_iota(jnp.int32, (rb, rb), 1) < lax.broadcasted_iota(jnp.int32, (rb, rb), 0), 1.0, 0.0)
+    before = dot(tri.astype(BF), both.astype(BF))
+
+    def place(oh, e):
+        slot = jnp.sum(before * oh, axis=1, keepdims=True).astype(jnp.int32)
+        ch = lax.shift_right_logical(slot, CH.bit_length() - 1)
+        return ch * (ne * CH) + e * CH + (slot - ch * CH)
+
+    code_ref[...] = jnp.where(lane == 0, place(oh0, e0), place(oh1, e1))
+    top[...] = jnp.zeros(top.shape, F32) + jnp.max(jnp.sum(both, axis=0, keepdims=True), axis=1, keepdims=True)
+    cnt[me] = top[...]
     for i, o in enumerate(others):
         dd, cc, tt = rel(*o)
-        rcopy(most_ref, cnt.at[me], n_s.at[i], n_r.at[me], dd, cc, tt).start()
+        rcopy(top, cnt.at[me], n_s.at[i], n_r.at[me], dd, cc, tt).start()
 
     zpeers = list(range(1, ncp))
 
@@ -108,6 +133,11 @@
 
     at_k = pl.multiple_of(k * rb, rb)
     at_c = pl.multiple_of((1 - k) * rb, rb)
+
+    ki = lax.broadcasted_iota(jnp.int32, (seg, seg), 0)
+    qi = lax.broadcasted_iota(jnp.int32, (seg, seg), 1)
+    bias[0] = jnp.zeros((seg, seg), F32)
+    bias[1] = jnp.where(ki <= qi, 0.0, NEG)
 
     for i in (0, 1, 2):
         loads[i].wait()
@@ -140,7 +170,7 @@
     c_dn = jnp.maximum(c - 1, 0)
 
     def wo_first():
-        rcopy(wo_hbm.at[piece(d, c)], wo_b.at[piece(d, c)], wy_s, wy_r, d, c, t_y).wait_recv()
+        wy.wait_recv()
         x_copy(c, False).start()
 
         @pl.when(c < ncp - 1)
@@ -151,27 +181,203 @@
         def _():
             dn_copy(c, c_dn).start()
 
-    def wo_next(i):
-        below = jnp.maximum(c - i, 0)
-        above = jnp.minimum(c + i, ncp - 1)
-
-        @pl.when(c - i >= 0)
+    def wo_near():
+        @pl.when(c > 0)
         def _():
-            up_copy(below, c_dn).wait_recv()
-
-            @pl.when(c < ncp - 1)
+            up_copy(c_dn, c_dn).wait_recv()
+
+            @pl.when(c == ncp - 2)
             def _():
-                up_copy(below, c_up).start()
-            x_copy(below, False).start()
-
-        @pl.when(c + i <= ncp - 1)
+                up_copy(c_dn, c_up).start()
+            x_copy(c_dn, False).start()
+
+        @pl.when(c < ncp - 1)
         def _():
-            dn_copy(above, c_up).wait_recv()
-
-            @pl.when(c > 0)
+            dn_copy(c_up, c_up).wait_recv()
+
+            @pl.when(c == 1)
             def _():
-                dn_copy(above, c_dn).start()
-            x_copy(above, False).start()
+                dn_copy(c_up, c_dn).start()
+            x_copy(c_up, False).start()
+
+    def wo_ends():
+        @pl.when(c == ncp - 1)
+        def _():
+            up_copy(ncp - 3, c_dn).wait_recv()
+            x_copy(ncp - 3, False).start()
+
+        @pl.when(c == 0)
+        def _():
+            dn_copy(2, c_up).wait_recv()
+            x_copy(2, False).start()
+
+    def wo_far():
+        wf.wait_recv()
+        x_copy(far, False).start()
+
+
+    zb, bk = xs.at[2:4], xs.at[0:2]
+    ff = wg_hbm.shape[1]
+    f1, f2 = wq.shape[1] // 4, w2buf.shape[2]
+    n1, n2 = ff // f1, hd // f2
+    self_e = c * ntp + t
+    rows = ne * CH
+    peers = [(dc, dt) for dc in [2, 1, 3, 0] for dt in range(ntp) if (dc, dt) != (0, 0)]
+
+    def blk(e):
+        return pl.ds(pl.multiple_of(e * CH, CH), CH)
+
+    def peer(dc, dt):
+        pc = lax.rem(c + dc, ncp)
+        pt = lax.rem(t + dt, ntp)
+        return pc, pt, pc * ntp + pt
+
+    def out_copy(j, dc, dt):
+        pc, pt, e = peer(dc, dt)
+        return rcopy(send.at[j, blk(e)], recv.at[j, blk(self_e)], ssem.at[j, e], rsem.at[j, self_e], d, pc, pt)
+
+    def in_copy(j, dc, dt):
+        pc, pt, e = peer(dc, dt)
+        return rcopy(send.at[j, blk(e)], recv.at[j, blk(e)], ssem.at[j, e], rsem.at[j, e], d, pc, pt)
+
+    def home_copy(j, dc, dt):
+        pc, pt, e = peer(dc, dt)
+        return rcopy(zb.at[j, blk(e)], bk.at[j, blk(self_e)], zsem.at[j, e], bsem.at[j, self_e], d, pc, pt)
+
+    def got_copy(j, dc, dt):
+        pc, pt, e = peer(dc, dt)
+        return rcopy(zb.at[j, blk(e)], bk.at[j, blk(e)], zsem.at[j, e], bsem.at[j, e], d, pc, pt)
+
+    def w1_copies(s):
+        slot = lax.rem(s, 2)
+        cols = pl.ds(pl.multiple_of(s * f1, f1), f1)
+        return (pltpu.make_async_copy(wg_hbm.at[:, cols], wq.at[:, pl.ds(pl.multiple_of(slot * 2 * f1, f1), f1)], w1sem.at[slot, 0]),
+                pltpu.make_async_copy(wu_hbm.at[:, cols], wq.at[:, pl.ds(pl.multiple_of(slot * 2 * f1 + f1, f1), f1)], w1sem.at[slot, 1]))
+
+    def w2_copy(s):
+        slot = lax.rem(s, 2)
+        cols = pl.ds(pl.multiple_of(s * f2, f2), f2)
+        return pltpu.make_async_copy(wd_hbm.at[:, cols], w2buf.at[slot], w2sem.at[slot])
+
+    def prefetch_w1():
+        for s in range(2):
+            for cp_ in w1_copies(jnp.int32(s)):
+                cp_.start()
+
+    def prefetch_w2():
+        for s in range(2):
+            w2_copy(jnp.int32(s)).start()
+
+    def dispatch():
+        for i in range(2):
+            rcopy(xs.at[t_y, half(i)], xs.at[t_y, half(i)], fx_s.at[i], fx_r.at[i], d, c, t_c).wait_send()
+        codes = code_ref[...].astype(F32).T.astype(jnp.int32)
+        for j in range(NCH):
+            ri = lax.broadcasted_iota(jnp.int32, (rows, rb), 0) + j * rows
+            sel = (jnp.where(ri == codes[0:1, :], 1.0, 0.0) + jnp.where(ri == codes[1:2, :], 1.0, 0.0)).astype(BF)
+
+            def pick(i, _):
+                cols = pl.ds(pl.multiple_of(i * 512, 512), 512)
+                send[j, :, cols] = dot(sel, h_ref[:, cols]).astype(BF)
+                return 0
+
+            lax.fori_loop(0, nc, pick, 0)
+            for dc, dt in peers:
+                out_copy(j, dc, dt).start()
+            recv[j, blk(self_e), :] = send[j, blk(self_e), :]
+
+    cw = seg // 2
+
+    def o_copy(j):
+        cols = pl.ds(pl.multiple_of(j * HD, HD), HD)
+        return rcopy(o_s.at[:, cols], o_b.at[:, cols], o_ss.at[j], o_rs.at[j], d, c, t_y)
+
+    def attend(hf, count, points):
+        n = count + 1
+
+        def following(j, g):
+            wrap = g == n - 1
+            return jnp.minimum(j + jnp.where(wrap, 1, 0), heads - 1), jnp.where(wrap, 0, g + 1)
+
+        def score(j, g, s_ref):
+            diag = jnp.where(g == n - 1, 1, 0)
+            qb = qq[hf, :, pl.ds(pl.multiple_of(j * HD, HD), HD)]
+            tops = []
+            for lo in range(0, seg, cw):
+                v = lax.dot_general(kb[g], qb[lo:lo + cw], (((1,), (1,)), ((), ())), preferred_element_type=F32) * scale
+                v = v + bias[diag, :, lo:lo + cw]
+                s_ref[:, lo:lo + cw] = v
+                tops.append(jnp.max(v, axis=0, keepdims=True))
+            return tuple(tops)
+
+        def soft(j, g, s_ref, tops, ms, ls):
+            first = g == 0
+            nm, nl = [], []
+            for n_, lo in enumerate(range(0, seg, cw)):
+                m = jnp.where(first, NEG, ms[n_])
+                mn = jnp.maximum(m, tops[n_])
+                w = jnp.exp(s_ref[:, lo:lo + cw] - mn)
+                a = jnp.exp(m - mn)
+                nl.append(jnp.where(first, 0.0, ls[n_]) * a + jnp.sum(w, axis=0, keepdims=True))
+                acc[:, lo:lo + cw] = acc[:, lo:lo + cw] * a + dot(vt[g], w.astype(BF))
+                nm.append(mn)
+            return tuple(nm), tuple(nl)
+
+        def finish(j, g, ls):
+            hcols = pl.ds(pl.multiple_of(j * HD, HD), HD)
+
+            @pl.when(g == n - 1)
+            def _():
+                for n_, lo in enumerate(range(0, seg, cw)):
+                    oo[hf, lo:lo + cw, hcols] = (acc[:, lo:lo + cw] / ls[n_]).T.astype(BF)
+
+            @pl.when((g == n - 1) & (hf == 1))
+            def _():
+                o_copy(j).start()
+
+        def pair(u, carry):
+            j0, g0, tops, ms, ls = carry
+            j1, g1 = following(j0, g0)
+            t1 = score(j1, g1, s1)
+            ms, ls = soft(j0, g0, s0, tops, ms, ls)
+            finish(j0, g0, ls)
+            j2, g2 = following(j1, g1)
+            t0 = score(j2, g2, s0)
+            ms, ls = soft(j1, g1, s1, t1, ms, ls)
+            finish(j1, g1, ls)
+            return j2, g2, t0, ms, ls
+
+        acc[...] = jnp.zeros(acc.shape, F32)
+        z1 = (jnp.zeros((1, cw), F32),) * 2
+        zero = jnp.int32(0)
+        total = heads * n
+        carry = (zero, zero, score(zero, zero, s0), z1, z1)
+        at = 0
+        for stop, point in points:
+            stop = jnp.minimum(stop, total // 2)
+            carry = lax.fori_loop(at, stop, pair, carry)
+            point()
+            at = stop
+        j, g, tops, ms, ls = lax.fori_loop(at, total // 2, pair, carry)
+
+        @pl.when(lax.rem(total, 2) == 1)
+        def _():
+            _, l2 = soft(j, g, s0, tops, ms, ls)
+            finish(j, g, l2)
+
+    def kv_wait(which):
+        for dc in zpeers:
+            cc = lax.rem(c + dc, ncp)
+            gm = jnp.where(y == 0, cc, last - cc)
+            go = last - gm
+            if which == 0:
+                parts = [(0, gm, at_k, rb), (1, gm, at_c, rb)]
+            else:
+                parts = [(2, go, at_k, hk), (3, go, pl.multiple_of(at_k + hk, hk), hk),
+                         (4, go, at_c, hk), (5, go, pl.multiple_of(at_c + hk, hk), hk)]
+            for i, g, at, n in parts:
+                for cp_ in kv_copies(g, at, n, i, dc, False):
+                    cp_.wait_recv()
 
     wo_first()
 
@@ -187,69 +393,32 @@
         kv_rows(other, a1, hk, xs[t_z, i * hk:(i + 1) * hk])
         kv_send(other, a1, hk, 4 + i)
         if i == 0:
-            wo_next(1)
+            wo_near()
     q_rows(q_b, at_k, xs[t_y])
     q_rows(q_b, at_c, xs[t_z])
 
-    for dc in zpeers:
-        cc = lax.rem(c + dc, ncp)
-        gm = jnp.where(y == 0, cc, last - cc)
-        go = last - gm
-        for i, (g, at, n) in enumerate([(gm, at_k, rb), (gm, at_c, rb),
-                                        (go, at_k, hk), (go, pl.multiple_of(at_k + hk, hk), hk),
-                                        (go, at_c, hk), (go, pl.multiple_of(at_c + hk, hk), hk)]):
-            for cp_ in kv_copies(g, at, n, i, dc, False):
-                cp_.wait_recv()
-
-    def step(g, carry, qb, masked):
-        m, l, acc = carry
-        s = lax.dot_general(kb[g], qb, (((1,), (1,)), ((), ())), preferred_element_type=F32) * scale
-        if masked:
-            ki = lax.broadcasted_iota(jnp.int32, s.shape, 0)
-            qi = lax.broadcasted_iota(jnp.int32, s.shape, 1)
-            s = jnp.where(ki <= qi, s, NEG)
-        mn = jnp.maximum(m, jnp.max(s, axis=0, keepdims=True))
-        w = jnp.exp(s - mn)
-        a = jnp.exp(m - mn)
-        l = l * a + jnp.sum(w, axis=0, keepdims=True)
-        acc = acc * a + dot(vt[g], w.astype(BF))
-        return mn, l, acc
-
-    def attend(q_ref, hcols, count):
-        qb = q_ref[:, hcols]
-        carry = (jnp.full((1, seg), NEG, F32), jnp.zeros((1, seg), F32), jnp.zeros((HD, seg), F32))
-        carry = lax.fori_loop(0, count, lambda g, cr: step(g, cr, qb, False), carry)
-        m, l, acc = step(count, carry, qb, True)
-        return (acc / l).T.astype(BF)
-
-    def o_copy(j):
-        cols = pl.ds(pl.multiple_of(j * HD, HD), HD)
-        return rcopy(o_s.at[:, cols], o_b.at[:, cols], o_ss.at[j], o_rs.at[j], d, c, t_y)
-
-    def head(j, _):
-        hcols = pl.ds(pl.multiple_of(j * HD, HD), HD)
-        o_s[:, hcols] = attend(q_b, hcols, other)
-        o_copy(j).start()
-        o_a[:, hcols] = attend(q_a, hcols, mine)
-        return 0
-
-    lax.fori_loop(0, 1, head, 0)
-    wo_next(2)
-    lax.fori_loop(1, 4, head, 0)
-    wo_next(3)
-    lax.fori_loop(4, heads, head, 0)
-
-    for cc in range(ncp):
-        x_copy(cc, True).wait_recv()
-    loads[4].wait()
-    for j in range(heads):
-        o_copy(j).wait_recv()
+    prefetch_w1()
+    prefetch_w2()
+    wo_ends()
+    kv_wait(0)
+    kv_wait(1)
+    attend(1, other, [(3, wo_far)])
+    attend(0, mine, [])
+
+    def finish_rows():
+        for cc in range(ncp):
+            x_copy(cc, True).wait_recv()
+        loads[4].wait()
+        for j in range(heads):
+            o_copy(j).wait_recv()
+        lax.fori_loop(0, nc, give, 0)
+        lax.fori_loop(0, nc, keep, 0)
+        dispatch()
 
     nc = hd // 512
-
     def p_copy(i):
         cols = pl.ds(pl.multiple_of(i * 512, 512), 512)
-        return rcopy(part.at[:, cols], pin.at[:, cols], p_ss.at[i], p_rs.at[i], d, c, t_c)
+        return rcopy(part.at[lax.rem(i, 2)], pin.at[:, cols], p_ss.at[i], p_rs.at[i], d, c, t_c)
 
     def proj(at, cols):
         rows = pl.ds(at, rb)
@@ -257,11 +426,14 @@
 
     def give(i, _):
         cols = pl.ds(pl.multiple_of(i * 512, 512), 512)
-        part[:, cols] = proj(at_c, cols)
+        v = proj(at_c, cols)
+
+        @pl.when(i >= 2)
+        def _():
+            p_copy(i - 2).wait_send()
+        part[lax.rem(i, 2)] = v
         p_copy(i).start()
         return 0
-
-    lax.fori_loop(0, nc, give, 0)
 
     def keep(i, _):
         cols = pl.ds(pl.multiple_of(i * 512, 512), 512)
@@ -270,22 +442,80 @@
         h_ref[:, cols] = (xs[t, :, cols].astype(F32) + (own + pin[:, cols])).astype(BF)
         return 0
 
-    lax.fori_loop(0, nc, keep, 0)
+
+    finish_rows()
+
+    for s in range(NCH):
+        for dc, dt in peers:
+            in_copy(s, dc, dt).wait_recv()
+
+        def up(i, _):
+            for cp_ in w1_copies(i):
+                cp_.wait()
+            at = pl.multiple_of(lax.rem(i, 2) * 2 * f1, f1)
+            xx = recv[s]
+            gg = dot(xx, wq[:, pl.ds(at, f1)])
+            uu = dot(xx, wq[:, pl.ds(pl.multiple_of(at + f1, f1), f1)])
+            act[:, pl.ds(pl.multiple_of(i * f1, f1), f1)] = (gg * jax.nn.sigmoid(gg) * uu).astype(BF)
+
+            @pl.when(i + 2 < n1)
+            def _():
+                for cp_ in w1_copies(i + 2):
+                    cp_.start()
+            return 0
+
+        lax.fori_loop(0, n1, up, 0)
+        if s + 1 < NCH:
+            prefetch_w1()
+
+        def down(i, _):
+            w2_copy(i).wait()
+            zb[s, :, pl.ds(pl.multiple_of(i * f2, f2), f2)] = dot(act[...], w2buf[lax.rem(i, 2)]).astype(BF)
+
+            @pl.when(i + 2 < n2)
+            def _():
+                w2_copy(i + 2).start()
+            return 0
+
+        lax.fori_loop(0, n2, down, 0)
+        if s + 1 < NCH:
+            prefetch_w2()
+        for dc, dt in peers:
+            home_copy(s, dc, dt).start()
+        bk[s, blk(self_e), :] = zb[s, blk(self_e), :]
+
+    for s in range(NCH):
+        for dc, dt in peers:
+            got_copy(s, dc, dt).wait_recv()
+
+    ci = lax.broadcasted_iota(jnp.int32, (rb, rows), 1)
+    sel0 = [jnp.where(ci + b_ * rows == code_ref[:, 0:1], 1.0, 0.0).astype(BF) for b_ in range(NCH)]
+    sel1 = [jnp.where(ci + b_ * rows == code_ref[:, 1:2], 1.0, 0.0).astype(BF) for b_ in range(NCH)]
+    g0 = g_ref[:, 0:1]
+    g1 = g_ref[:, 1:2]
+
+    def combine(i, _):
+        cols = pl.ds(pl.multiple_of(i * 512, 512), 512)
+        z0 = dot(sel0[0], bk[0, :, cols]) + dot(sel0[1], bk[1, :, cols])
+        z1 = dot(sel1[0], bk[0, :, cols]) + dot(sel1[1], bk[1, :, cols])
+        y_ref[:, cols] = (h_ref[:, cols].astype(F32) + (g0 * z0 + g1 * z1)).astype(BF)
+        return 0
+
+    lax.fori_loop(0, nc, combine, 0)
 
     for o in others:
         dd, cc, tt = rel(*o)
         src = (dd * ncp + cc) * ntp + tt
-        rcopy(most_ref, cnt.at[src], n_s.at[0], n_r.at[src], dd, cc, tt).wait_recv()
+        rcopy(top, cnt.at[src], n_s.at[0], n_r.at[src], dd, cc, tt).wait_recv()
     mx_ref[...] = jnp.max(cnt[...], axis=0)
 
     wy.wait_send()
     cx.wait_send()
     for i in range(2):
         yx[i].wait_send()
-        rcopy(xs.at[t_y, half(i)], xs.at[t_y, half(i)], fx_s.at[i], fx_r.at[i], d, c, t_c).wait_send()
     for i, o in enumerate(others):
         dd, cc, tt = rel(*o)
-        rcopy(most_ref, cnt.at[me], n_s.at[i], n_r.at[me], dd, cc, tt).wait_send()
+        rcopy(top, cnt.at[me], n_s.at[i], n_r.at[me], dd, cc, tt).wait_send()
     for dc in zpeers:
         for i, (g, at, n) in enumerate([(mine, at_k, rb), (mine, at_c, rb),
                                         (other, at_k, hk), (other, pl.multiple_of(at_k + hk, hk), hk),
@@ -295,52 +525,70 @@
     for cc in range(ncp):
         x_copy(cc, False).wait_send()
 
-        @pl.when((cc <= c) & (c < ncp - 1))
-        def _():
-            up_copy(cc, c_up).wait_send()
-
-        @pl.when((cc >= c) & (c > 0))
-        def _():
-            dn_copy(cc, c_dn).wait_send()
+
+    @pl.when(c < ncp - 1)
+    def _():
+        up_copy(c, c_up).wait_send()
+
+    @pl.when(c > 0)
+    def _():
+        dn_copy(c, c_dn).wait_send()
+
+    @pl.when(c == ncp - 2)
+    def _():
+        up_copy(c_dn, c_up).wait_send()
+
+    @pl.when(c == 1)
+    def _():
+        dn_copy(c_up, c_dn).wait_send()
+    wf.wait_send()
     for j in range(heads):
         o_copy(j).wait_send()
-    for i in range(nc):
+    for i in (nc - 2, nc - 1):
         p_copy(i).wait_send()
-
-
-def attention(x, wq, wk, wv, wo, most, *, nd, ncp, ntp, cid):
+    for j in range(NCH):
+        for dc, dt in peers:
+            out_copy(j, dc, dt).wait_send()
+            home_copy(j, dc, dt).wait_send()
+
+
+def layer(x, wq, wk, wv, wo, idx, gates, wg, wu, wd, *, nd, ncp, ntp, cid):
     rb, hd = x.shape
     ql = wq.shape[1]
     seg = 2 * rb
     heads = ql // HD
     nseg = 2 * ncp
     n_all = nd * ncp * ntp
+    ne = ncp * ntp
+    ff = wg.shape[1]
     hbm = pl.BlockSpec(memory_space=pl.ANY)
     vm = pl.BlockSpec(memory_space=pltpu.VMEM)
     dma = pltpu.SemaphoreType.DMA
     V = pltpu.VMEM
     return pl.pallas_call(
-        functools.partial(att_kernel, nd=nd, ncp=ncp, ntp=ntp, scale=HD ** -0.5),
-        in_specs=[hbm, hbm, hbm, hbm, hbm, vm],
-        out_specs=[vm, vm],
-        out_shape=[jax.ShapeDtypeStruct((rb, hd), BF), jax.ShapeDtypeStruct(most.shape, most.dtype)],
+        functools.partial(layer_kernel, nd=nd, ncp=ncp, ntp=ntp, scale=HD ** -0.5),
+        in_specs=[hbm, hbm, hbm, hbm, hbm, vm, vm, hbm, hbm, hbm],
+        out_specs=[vm, vm, vm, vm],
+        out_shape=[jax.ShapeDtypeStruct((rb, hd), BF), jax.ShapeDtypeStruct((rb, hd), BF), jax.ShapeDtypeStruct((rb, 128), jnp.int32), jax.ShapeDtypeStruct((8, 128), F32)],
         scratch_shapes=[
-            V((ntp, rb, hd), BF), V((hd, ql), BF), V((hd, 2 * HD), BF), V((ql, hd), BF), V((ql, hd), BF),
-            V((seg, ql), BF), V((seg, ql), BF), V((nseg, seg, HD), BF), V((nseg, HD, seg), BF),
-            V((seg, ql), BF), V((seg, ql), BF), V((seg, ql), BF), V((rb, hd), F32), V((rb, hd), F32),
-            V((n_all,) + most.shape, most.dtype),
+            V((ntp, rb, hd), BF), V((hd, 1024), BF), V((hd, 2 * HD), BF), V((ql, hd), BF), V((ql, hd), BF),
+            V((2, seg, ql), BF), V((nseg, seg, HD), BF), V((nseg, HD, seg), BF),
+            V((2, seg, ql), BF), V((seg, ql), BF), V((2, rb, 512), F32), V((rb, hd), F32),
+            V((n_all, 8, 128), F32), V((8, 128), F32), V((seg, seg), F32), V((seg, seg), F32), V((2, seg, seg), F32), V((HD, seg), F32),
+            V((NCH, ne * CH, hd), BF), V((NCH, ne * CH, hd), BF), V((ne * CH, ff), BF), V((2, ff, 256), BF),
             dma((5,)), dma(()), dma(()), dma((2,)), dma((2,)), dma((2,)), dma((2,)),
             dma((ncp, 12)), dma((ncp, 12)), dma(()), dma(()), dma((ncp,)), dma((ncp,)),
-            dma((ncp,)), dma((ncp,)), dma((ncp,)), dma((ncp,)), dma((heads,)), dma((heads,)),
+            dma((ncp,)), dma((ncp,)), dma((ncp,)), dma((ncp,)), dma(()), dma(()), dma((heads,)), dma((heads,)),
             dma((hd // 512,)), dma((hd // 512,)), dma((n_all - 1,)), dma((n_all,)),
+            dma((NCH, ne)), dma((NCH, ne)), dma((NCH, ne)), dma((NCH, ne)), dma((2, 2)), dma((2,)),
         ],
         compiler_params=pltpu.CompilerParams(collective_id=cid, has_side_effects=True, vmem_limit_bytes=VMEM_LIMIT),
-        name="att",
+        name="layer",
         cost_estimate=pl.CostEstimate(flops=60_000_000_000, bytes_accessed=30_000_000, transcendentals=0),
-    )(x, wq, wk, wv, wo, most)
-
-
-def moe_kernel(h_ref, dr_ref, dc_ref, g_ref, wg_hbm, wu_hbm, wd_hbm, y_ref,
+    )(x, wq, wk, wv, wo, idx, gates, wg, wu, wd)
+
+
+def moe_kernel(h_ref, dc_ref, g_ref, wg_hbm, wu_hbm, wd_hbm, y_ref,
                send, recv, zbuf, back, act, w1buf, w2buf,
                ssem, rsem, zsem, bsem, w1sem, w2sem, *, ncp, ntp, nch, f1, f2):
     ne = ncp * ntp
@@ -417,9 +665,11 @@
         pl.semaphore_signal(barrier, inc=1, device_id=(dp, pc, pt), device_id_type=MESH)
     pl.semaphore_wait(barrier, ne - 1)
 
+    codes = dc_ref[...].astype(F32).T.astype(jnp.int32)
+
     for j in range(nch):
         ri = lax.broadcasted_iota(jnp.int32, (rows, t), 0) + j * rows
-        sel = jnp.where(ri == dr_ref[0:1, :], 1.0, 0.0) + jnp.where(ri == dr_ref[1:2, :], 1.0, 0.0)
+        sel = jnp.where(ri == codes[0:1, :], 1.0, 0.0) + jnp.where(ri == codes[1:2, :], 1.0, 0.0)
         sel = sel.astype(BF)
 
         def pick(i, _):
@@ -496,7 +746,7 @@
             home_copy(j, dc, dt).wait_send()
 
 
-def moe(h, drow, dcol, gates, wg, wu, wd, *, ncp, ntp, nch, cid):
+def moe(h, code, gates, wg, wu, wd, *, ncp, ntp, nch, cid):
     t, hd = h.shape
     ff = wg.shape[1]
     ne = ncp * ntp
@@ -507,7 +757,7 @@
     dma = pltpu.SemaphoreType.DMA
     return pl.pallas_call(
         functools.partial(moe_kernel, ncp=ncp, ntp=ntp, nch=nch, f1=f1, f2=f2),
-        in_specs=[vm, vm, vm, vm, hbm, hbm, hbm],
+        in_specs=[vm, vm, vm, hbm, hbm, hbm],
         out_specs=vm,
         out_shape=jax.ShapeDtypeStruct((t, hd), BF),
         scratch_shapes=[
@@ -521,42 +771,24 @@
         compiler_params=pltpu.CompilerParams(collective_id=cid, has_side_effects=True, vmem_limit_bytes=VMEM_LIMIT),
         name=f"moe{nch}",
         cost_estimate=pl.CostEstimate(flops=6 * nch * rows * hd * ff, bytes_accessed=6 * nch * hd * ff, transcendentals=0),
-    )(h, drow, dcol, gates, wg, wu, wd)
-
-
-def route(idx, ne):
-    t = idx.shape[0]
-    e = jnp.arange(ne, dtype=jnp.int32)[None, :]
-    oh0 = (idx[:, 0:1] == e).astype(F32)
-    oh1 = (idx[:, 1:2] == e).astype(F32)
-    both = oh0 + oh1
-    i = jnp.arange(t)
-    before = dot((i[None, :] < i[:, None]).astype(F32), both)
-    s0 = jnp.sum(before * oh0, axis=1).astype(jnp.int32)
-    s1 = jnp.sum(before * oh1, axis=1).astype(jnp.int32)
-    slot = jnp.stack([s0, s1], axis=1)
-    code = (slot // CH) * (ne * CH) + idx * CH + slot % CH
-    return code, jnp.max(jnp.sum(both, axis=0)).astype(jnp.int32)
+    )(h, code, gates, wg, wu, wd)
 
 
 def solution(mesh):
     ncp = mesh.shape["cp"]
     ntp = mesh.shape["tp"]
-    ne = ncp * ntp
     rows_spec = P(("dp", "cp", "tp"), None)
     exp_spec = P(("cp", "tp"), None, None)
 
     def local(x, idx, gates, wq, wk, wv, wo, w1g, w1u, w2):
-        code, most = route(idx, ne)
-        drow = jnp.pad(code.T, ((0, 6), (0, 0)))
-        h, most = attention(x, wq, wk, wv, wo, jnp.full((8, 128), most), nd=mesh.shape["dp"], ncp=ncp, ntp=ntp, cid=3)
+        y, h, code, most = layer(x, wq, wk, wv, wo, idx, gates, w1g[0], w1u[0], w2[0], nd=mesh.shape["dp"], ncp=ncp, ntp=ntp, cid=3)
 
         def few(args):
-            return moe(*args, ncp=ncp, ntp=ntp, nch=2, cid=1)
+            return y
 
         def many(args):
             return moe(*args, ncp=ncp, ntp=ntp, nch=4, cid=2)
 
-        return lax.cond(most[0, 0] <= 2 * CH, few, many, (h, drow, code, gates, w1g[0], w1u[0], w2[0]))
+        return lax.cond(most[0, 0] <= NCH * CH, few, many, (h, code, gates, w1g[0], w1u[0], w2[0]))
 
     return jax.shard_map(local, mesh=mesh, in_specs=(rows_spec, rows_spec, rows_spec, P(None, "tp"), P(None, "tp"), P(None, "tp"), P("tp", None), exp_spec, exp_spec, exp_spec), out_specs=rows_spec, check_vma=False)

time: 496 us -> 631 us (1.27)
  Pallas kernels: 484 us -> 622 us
    pallas_call x1, Pallas kernels: 147 us -> 289 us  [layer(): pl.pallas_call(functools.partial(layer_kernel, nd=nd, ncp=ncp, ntp=ntp, s...]
where the time goes in v3:
time: 631 us; the launch traced here: 630 us
  Pallas kernels  622 us (99%)
  local copies, waits for them, and re-layouts  7.78 us (1%)
    pallas_call x1, Pallas kernels, moe(): pl.pallas_call(functools.partial(moe_kernel, ncp=ncp, ntp=ntp, nch=nch, f...  333 us
    pallas_call x1, Pallas kernels, layer(): pl.pallas_call(functools.partial(layer_kernel, nd=nd, ncp=ncp, ntp=ntp, s...  289 us

profile of v3, /device:TPU:9, one launch (start us, length us, event | category | flops | bytes accessed | tf_op | source)
XLA Modules:
  0.0 630.5 jit_solution(717211352120996838)
XLA Ops:
  0.0 1.5 copy.13.idx_ref
  1.5 1.5 copy.14.g_ref
  2.9 0.0 copy-start
  2.9 289.2 %layer.1 = (bf16[256,3584]{1,0:T(8,128)(2,1)}, bf16[256,3584]{1,0:T(8,128)(2,1)}, s32[256,128]{1,0:T(8,128)}, f32[8,128]{1,0:T(8,128)}) custom-call(bf16[256,3584]{1,0:T(8,128)(2,1)} %x_hbm.1, bf16[3584,896]{1,0:T(8,128)(2,1)} %wq_hbm.1, bf16[3584,128]{1,0:T(8,128)(2,1)} %wk_hbm.1, bf16[3584,128]{1,0:T(8,128)(2,1)} %wv_hbm.1, bf16[896,3584]{1,0:T(8,128)(2,1)} %wo_hbm.1, ...), custom_call_target="tpu_custom_call" | custom-call | flops 60000002048 | bytes 30000000 | tf_op jit(solution)/shard_map/layer/pallas_call | solution.py:568
  292.1 1.2 slice.3
  294.0 0.0 copy-done
  294.0 333.6 %conditional.1 = (bf16[256,3584]{1,0:T(8,128)(2,1)}) conditional(s32[]{:T(128)} %bitcast.3, (bf16[256,3584]{1,0:T(8,128)(2,1)}, s32[256,128]{1,0:T(8,128)}, f32[256,2]{0,1:T(2,128)S(1)}, bf16[3584,2560]{1,0:T(8,128)(2,1)}, bf16[3584,2560]{1,0:T(8,128)(2,1)}, /*index=5*/bf16[2560,3584]{1,0:T(8,128)(2,1)}) %tuple.21, ...), branch_computations={%region_0.0_spmd, %region_1.0_spmd} | conditional | flops 56371445760 | bytes 220205056 | solution.py:792
  294.2 0.8 copy.15.g_ref
  295.0 332.6 %moe4.1 = bf16[256,3584]{1,0:T(8,128)(2,1)} custom-call(bf16[256,3584]{1,0:T(8,128)(2,1)} %get-tuple-element.21.h_ref, s32[256,128]{1,0:T(8,128)} %get-tuple-element.22.dc_ref, f32[256,2]{1,0:T(8,128)} %copy.15.g_ref, bf16[3584,2560]{1,0:T(8,128)(2,1)} %get-tuple-element.24.wg_hbm, bf16[3584,2560]{1,0:T(8,128)(2,1)} %get-tuple-element.25.wu_hbm, ...), custom_call_target="tpu_custom_call" | custom-call | flops 56371445760 | bytes 220200960 | tf_op jit(solution)/shard_map/cond/branch_0_fun/moe4/pallas_call | solution.py:758
  627.6 2.8 copy.19
Async XLA Ops:
  2.9 291.0 %copy-start = (f32[256,2]{0,1:T(2,128)S(1)}, f32[256,2]{0,1:T(2,128)}, u32[]{:S(2)}) copy-start(f32[256,2]{0,1:T(2,128)} %param.14) | copy-start | bytes 6148

commit v4 on v3

--- a/solution.py
+++ b/solution.py
@@ -26,7 +26,7 @@
                xs, wq, wkv, wo_a, wo_b, qq, kb, vt, oo, o_b, part, pin, cnt, top, s0, s1, bias, acc,
                send, recv, act, w2buf,
                lsem, cx_s, cx_r, yx_s, yx_r, fx_s, fx_r, kv_s, kv_r, wy_s, wy_r, wx_s, wx_r,
-               wu_s, wu_r, wd_s, wd_r, wf_s, wf_r, o_ss, o_rs, p_ss, p_rs, n_s, n_r, ssem, rsem, zsem, bsem, w1sem, w2sem, *, nd, ncp, ntp, scale):
+               wu_s, wu_r, wd_s, wd_r, wf_s, wf_r, wc_s, wc_r, o_ss, o_rs, p_ss, p_rs, n_s, n_r, ssem, rsem, zsem, bsem, w1sem, w2sem, *, nd, ncp, ntp, scale):
     d = lax.axis_index("dp")
     c = lax.axis_index("cp")
     t = lax.axis_index("tp")
@@ -77,15 +77,22 @@
     def half(i):
         return pl.ds(i * hk, hk)
 
-    wy = rcopy(wo_hbm.at[piece(d, c)], wo_b.at[piece(d, c)], wy_s, wy_r, d, c, t_y)
+    def cols2(v):
+        return pl.ds(v * (hd // 2), hd // 2)
+
+    def wo_cut(ref, dd, cc, v):
+        return ref.at[piece(dd, cc), cols2(v)]
+
+    wy = [rcopy(wo_cut(wo_hbm, d, c, v), wo_cut(wo_b, d, c, v), wy_s.at[v], wy_r.at[v], d, c, t_y) for v in range(2)]
     yx = [rcopy(x_hbm.at[half(i)], xs.at[t, half(i)], yx_s.at[i], yx_r.at[i], d, c, t_y) for i in range(2)]
     yx_in = [rcopy(x_hbm.at[half(i)], xs.at[t_y, half(i)], yx_s.at[i], yx_r.at[i], d, c, t_y) for i in range(2)]
     far = jnp.where(c < ncp // 2, ncp - 1, 0)
     wf = rcopy(wo_hbm.at[piece(d, far)], wo_b.at[piece(d, far)], wf_s, wf_r, d, c, t_y)
 
-    wy.start()
+    wy[0].start()
     for cp_ in yx:
         cp_.start()
+    wy[1].start()
     wf.start()
     cx = rcopy(x_hbm, xs.at[t], cx_s, cx_r, d, c, t_c)
     cx_in = rcopy(x_hbm, xs.at[t_c], cx_s, cx_r, d, c, t_c)
@@ -93,7 +100,11 @@
 
     ne = ncp * ntp
     lane = lax.broadcasted_iota(jnp.int32, (rb, 128), 1)
-    e0, e1 = idx_ref[:, 0:1], idx_ref[:, 1:2]
+
+    def column(ref, i):
+        return jnp.broadcast_to(ref[i:i + 1, :].astype(F32), (128, rb)).T
+
+    e0, e1 = column(idx_ref, 0).astype(jnp.int32), column(idx_ref, 1).astype(jnp.int32)
     oh0 = jnp.where(lane == e0, 1.0, 0.0)
     oh1 = jnp.where(lane == e1, 1.0, 0.0)
     both = oh0 + oh1
@@ -156,64 +167,84 @@
     q_rows(q_a, at_k, xs[t])
     q_rows(q_a, at_c, xs[t_c])
 
-    def x_copy(cc, there):
+    def x_copy(cc, there, v):
         dd = 1 - d if there else d
-        return rcopy(wo_b.at[piece(dd, cc)], wo_b.at[piece(dd, cc)], wx_s.at[cc], wx_r.at[cc], 1 - d, c, t)
-
-    def up_copy(cc, to):
-        return rcopy(wo_b.at[piece(d, cc)], wo_b.at[piece(d, cc)], wu_s.at[cc], wu_r.at[cc], d, to, t)
-
-    def dn_copy(cc, to):
-        return rcopy(wo_b.at[piece(d, cc)], wo_b.at[piece(d, cc)], wd_s.at[cc], wd_r.at[cc], d, to, t)
+        return rcopy(wo_cut(wo_b, dd, cc, v), wo_cut(wo_b, dd, cc, v), wx_s.at[cc, v], wx_r.at[cc, v], 1 - d, c, t)
+
+    def up_copy(cc, to, v):
+        return rcopy(wo_cut(wo_b, d, cc, v), wo_cut(wo_b, d, cc, v), wu_s.at[cc, v], wu_r.at[cc, v], d, to, t)
+
+    def dn_copy(cc, to, v):
+        return rcopy(wo_cut(wo_b, d, cc, v), wo_cut(wo_b, d, cc, v), wd_s.at[cc, v], wd_r.at[cc, v], d, to, t)
+
+    def up2_copy(cc, to):
+        return rcopy(wo_cut(wo_b, 1 - d, cc, 1), wo_cut(wo_b, 1 - d, cc, 1), wc_s.at[0], wc_r.at[0], d, to, t)
+
+    def dn2_copy(cc, to):
+        return rcopy(wo_cut(wo_b, 1 - d, cc, 1), wo_cut(wo_b, 1 - d, cc, 1), wc_s.at[1], wc_r.at[1], d, to, t)
 
     c_up = jnp.minimum(c + 1, ncp - 1)
     c_dn = jnp.maximum(c - 1, 0)
 
-    def wo_first():
-        wy.wait_recv()
-        x_copy(c, False).start()
+    def wo_first(v):
+        wy[v].wait_recv()
+        x_copy(c, False, v).start()
 
         @pl.when(c < ncp - 1)
         def _():
-            up_copy(c, c_up).start()
+            up_copy(c, c_up, v).start()
 
         @pl.when(c > 0)
         def _():
-            dn_copy(c, c_dn).start()
-
-    def wo_near():
+            dn_copy(c, c_dn, v).start()
+
+    def wo_near(v):
         @pl.when(c > 0)
         def _():
-            up_copy(c_dn, c_dn).wait_recv()
+            up_copy(c_dn, c_dn, v).wait_recv()
 
             @pl.when(c == ncp - 2)
             def _():
-                up_copy(c_dn, c_up).start()
-            x_copy(c_dn, False).start()
+                up_copy(c_dn, c_up, v).start()
+            if v == 0:
+                x_copy(c_dn, False, v).start()
 
         @pl.when(c < ncp - 1)
         def _():
-            dn_copy(c_up, c_up).wait_recv()
+            dn_copy(c_up, c_up, v).wait_recv()
 
             @pl.when(c == 1)
             def _():
-                dn_copy(c_up, c_dn).start()
-            x_copy(c_up, False).start()
-
-    def wo_ends():
+                dn_copy(c_up, c_dn, v).start()
+            if v == 0:
+                x_copy(c_up, False, v).start()
+
+    def wo_cross():
+        x_copy(c, True, 1).wait_recv()
+
+        @pl.when(c < ncp - 1)
+        def _():
+            up2_copy(c, c_up).start()
+
+        @pl.when(c > 0)
+        def _():
+            dn2_copy(c, c_dn).start()
+
+    def wo_ends(v):
         @pl.when(c == ncp - 1)
         def _():
-            up_copy(ncp - 3, c_dn).wait_recv()
-            x_copy(ncp - 3, False).start()
+            up_copy(ncp - 3, c_dn, v).wait_recv()
+            x_copy(ncp - 3, False, v).start()
 
         @pl.when(c == 0)
         def _():
-            dn_copy(2, c_up).wait_recv()
-            x_copy(2, False).start()
+            dn_copy(2, c_up, v).wait_recv()
+            x_copy(2, False, v).start()
 
     def wo_far():
         wf.wait_recv()
-        x_copy(far, False).start()
+        for v in range(2):
+            x_copy(far, False, v).start()
 
 
     zb, bk = xs.at[2:4], xs.at[0:2]
@@ -353,10 +384,10 @@
         total = heads * n
         carry = (zero, zero, score(zero, zero, s0), z1, z1)
         at = 0
-        for stop, point in points:
+        for stop, here, point in points:
             stop = jnp.minimum(stop, total // 2)
             carry = lax.fori_loop(at, stop, pair, carry)
-            point()
+            pl.when(here)(point)
             at = stop
         j, g, tops, ms, ls = lax.fori_loop(at, total // 2, pair, carry)
 
@@ -379,7 +410,7 @@
                 for cp_ in kv_copies(g, at, n, i, dc, False):
                     cp_.wait_recv()
 
-    wo_first()
+    wo_first(0)
 
     for i in range(2):
         yx_in[i].wait_recv()
@@ -393,21 +424,41 @@
         kv_rows(other, a1, hk, xs[t_z, i * hk:(i + 1) * hk])
         kv_send(other, a1, hk, 4 + i)
         if i == 0:
-            wo_near()
+            wo_near(0)
     q_rows(q_b, at_k, xs[t_y])
     q_rows(q_b, at_c, xs[t_z])
 
     prefetch_w1()
     prefetch_w2()
-    wo_ends()
+    wo_ends(0)
     kv_wait(0)
+    wo_first(1)
     kv_wait(1)
-    attend(1, other, [(3, wo_far)])
-    attend(0, mine, [])
+    points = [(4, wo_cross), (5, lambda: wo_near(1)), (13, wo_far), (20, lambda: wo_ends(1))]
+    done = heads * (other + 1) // 2
+    attend(1, other, [(stop, stop <= done, point) for stop, point in points])
+    attend(0, mine, [(jnp.maximum(stop - done, 0), stop > done, point) for stop, point in points])
 
     def finish_rows():
         for cc in range(ncp):
-            x_copy(cc, True).wait_recv()
+            x_copy(cc, True, 0).wait_recv()
+        x_copy(far, True, 1).wait_recv()
+
+        @pl.when(c == 0)
+        def _():
+            x_copy(2, True, 1).wait_recv()
+
+        @pl.when(c == ncp - 1)
+        def _():
+            x_copy(ncp - 3, True, 1).wait_recv()
+
+        @pl.when(c > 0)
+        def _():
+            up2_copy(c_dn, c_dn).wait_recv()
+
+        @pl.when(c < ncp - 1)
+        def _():
+            dn2_copy(c_up, c_up).wait_recv()
         loads[4].wait()
         for j in range(heads):
             o_copy(j).wait_recv()
@@ -484,24 +535,27 @@
             home_copy(s, dc, dt).start()
         bk[s, blk(self_e), :] = zb[s, blk(self_e), :]
 
+    ci = lax.broadcasted_iota(jnp.int32, (rb, rows), 1)
+    g0 = column(g_ref, 0)[:, 0:1]
+    g1 = column(g_ref, 1)[:, 0:1]
     for s in range(NCH):
+        sel0 = jnp.where(ci + s * rows == code_ref[:, 0:1], 1.0, 0.0).astype(BF)
+        sel1 = jnp.where(ci + s * rows == code_ref[:, 1:2], 1.0, 0.0).astype(BF)
         for dc, dt in peers:
             got_copy(s, dc, dt).wait_recv()
 
-    ci = lax.broadcasted_iota(jnp.int32, (rb, rows), 1)
-    sel0 = [jnp.where(ci + b_ * rows == code_ref[:, 0:1], 1.0, 0.0).astype(BF) for b_ in range(NCH)]
-    sel1 = [jnp.where(ci + b_ * rows == code_ref[:, 1:2], 1.0, 0.0).astype(BF) for b_ in range(NCH)]
-    g0 = g_ref[:, 0:1]
-    g1 = g_ref[:, 1:2]
-
-    def combine(i, _):
-        cols = pl.ds(pl.multiple_of(i * 512, 512), 512)
-        z0 = dot(sel0[0], bk[0, :, cols]) + dot(sel0[1], bk[1, :, cols])
-        z1 = dot(sel1[0], bk[0, :, cols]) + dot(sel1[1], bk[1, :, cols])
-        y_ref[:, cols] = (h_ref[:, cols].astype(F32) + (g0 * z0 + g1 * z1)).astype(BF)
-        return 0
-
-    lax.fori_loop(0, nc, combine, 0)
+        def combine(i, _):
+            cols = pl.ds(pl.multiple_of(i * 512, 512), 512)
+            v = g0 * dot(sel0, bk[s, :, cols]) + g1 * dot(sel1, bk[s, :, cols])
+            if s > 0:
+                v = pin[:, cols] + v
+            if s + 1 < NCH:
+                pin[:, cols] = v
+            else:
+                y_ref[:, cols] = (h_ref[:, cols].astype(F32) + v).astype(BF)
+            return 0
+
+        lax.fori_loop(0, nc, combine, 0)
 
     for o in others:
         dd, cc, tt = rel(*o)
@@ -509,7 +563,8 @@
         rcopy(top, cnt.at[src], n_s.at[0], n_r.at[src], dd, cc, tt).wait_recv()
     mx_ref[...] = jnp.max(cnt[...], axis=0)
 
-    wy.wait_send()
+    for v in range(2):
+        wy[v].wait_send()
     cx.wait_send()
     for i in range(2):
         yx[i].wait_send()
@@ -523,24 +578,43 @@
             for cp_ in kv_copies(g, at, n, i, dc, True):
                 cp_.wait_send()
     for cc in range(ncp):
-        x_copy(cc, False).wait_send()
-
+        x_copy(cc, False, 0).wait_send()
+    x_copy(c, False, 1).wait_send()
+    x_copy(far, False, 1).wait_send()
+
+    @pl.when(c == 0)
+    def _():
+        x_copy(2, False, 1).wait_send()
+
+    @pl.when(c == ncp - 1)
+    def _():
+        x_copy(ncp - 3, False, 1).wait_send()
 
     @pl.when(c < ncp - 1)
     def _():
-        up_copy(c, c_up).wait_send()
+        up2_copy(c, c_up).wait_send()
 
     @pl.when(c > 0)
     def _():
-        dn_copy(c, c_dn).wait_send()
-
-    @pl.when(c == ncp - 2)
-    def _():
-        up_copy(c_dn, c_up).wait_send()
-
-    @pl.when(c == 1)
-    def _():
-        dn_copy(c_up, c_dn).wait_send()
+        dn2_copy(c, c_dn).wait_send()
+
+    for v in range(2):
+
+        @pl.when(c < ncp - 1)
+        def _():
+            up_copy(c, c_up, v).wait_send()
+
+        @pl.when(c > 0)
+        def _():
+            dn_copy(c, c_dn, v).wait_send()
+
+        @pl.when(c == ncp - 2)
+        def _():
+            up_copy(c_dn, c_up, v).wait_send()
+
+        @pl.when(c == 1)
+        def _():
+            dn_copy(c_up, c_dn, v).wait_send()
     wf.wait_send()
     for j in range(heads):
         o_copy(j).wait_send()
@@ -577,15 +651,15 @@
             V((n_all, 8, 128), F32), V((8, 128), F32), V((seg, seg), F32), V((seg, seg), F32), V((2, seg, seg), F32), V((HD, seg), F32),
             V((NCH, ne * CH, hd), BF), V((NCH, ne * CH, hd), BF), V((ne * CH, ff), BF), V((2, ff, 256), BF),
             dma((5,)), dma(()), dma(()), dma((2,)), dma((2,)), dma((2,)), dma((2,)),
-            dma((ncp, 12)), dma((ncp, 12)), dma(()), dma(()), dma((ncp,)), dma((ncp,)),
-            dma((ncp,)), dma((ncp,)), dma((ncp,)), dma((ncp,)), dma(()), dma(()), dma((heads,)), dma((heads,)),
+            dma((ncp, 12)), dma((ncp, 12)), dma((2,)), dma((2,)), dma((ncp, 2)), dma((ncp, 2)),
+            dma((ncp, 2)), dma((ncp, 2)), dma((ncp, 2)), dma((ncp, 2)), dma(()), dma(()), dma((2,)), dma((2,)), dma((heads,)), dma((heads,)),
             dma((hd // 512,)), dma((hd // 512,)), dma((n_all - 1,)), dma((n_all,)),
             dma((NCH, ne)), dma((NCH, ne)), dma((NCH, ne)), dma((NCH, ne)), dma((2, 2)), dma((2,)),
         ],
         compiler_params=pltpu.CompilerParams(collective_id=cid, has_side_effects=True, vmem_limit_bytes=VMEM_LIMIT),
         name="layer",
         cost_estimate=pl.CostEstimate(flops=60_000_000_000, bytes_accessed=30_000_000, transcendentals=0),
-    )(x, wq, wk, wv, wo, idx, gates, wg, wu, wd)
+    )(x, wq, wk, wv, wo, idx.T, gates.T, wg, wu, wd)
 
 
 def moe_kernel(h_ref, dc_ref, g_ref, wg_hbm, wu_hbm, wd_hbm, y_ref,

time: 631 us -> 622 us (0.986)
  Pallas kernels: 622 us -> 615 us
where the time goes in v4:
time: 622 us; the launch traced here: 621 us
  Pallas kernels  615 us (99%)
    pallas_call x1, Pallas kernels, moe(): pl.pallas_call(functools.partial(moe_kernel, ncp=ncp, ntp=ntp, nch=nch, f...  332 us
    pallas_call x1, Pallas kernels, layer(): pl.pallas_call(functools.partial(layer_kernel, nd=nd, ncp=ncp, ntp=ntp, s...  283 us

profile of v4, /device:TPU:9, one launch (start us, length us, event | category | flops | bytes accessed | tf_op | source)
XLA Modules:
  0.0 621.0 jit_solution(2925526168857943118)
XLA Ops:
  0.0 0.0 copy-start
  0.0 283.1 %layer.1 = (bf16[256,3584]{1,0:T(8,128)(2,1)}, bf16[256,3584]{1,0:T(8,128)(2,1)}, s32[256,128]{1,0:T(8,128)}, f32[8,128]{1,0:T(8,128)}) custom-call(bf16[256,3584]{1,0:T(8,128)(2,1)} %x_hbm.1, bf16[3584,896]{1,0:T(8,128)(2,1)} %wq_hbm.1, bf16[3584,128]{1,0:T(8,128)(2,1)} %wk_hbm.1, bf16[3584,128]{1,0:T(8,128)(2,1)} %wv_hbm.1, bf16[896,3584]{1,0:T(8,128)(2,1)} %wo_hbm.1, ...), custom_call_target="tpu_custom_call" | custom-call | flops 60000002048 | bytes 30000000 | tf_op jit(solution)/shard_map/layer/pallas_call | solution.py:642
  283.1 1.2 slice.3
  285.0 0.0 copy-done
  285.0 333.2 %conditional.1 = (bf16[256,3584]{1,0:T(8,128)(2,1)}) conditional(s32[]{:T(128)} %bitcast.5, (bf16[256,3584]{1,0:T(8,128)(2,1)}, s32[256,128]{1,0:T(8,128)}, f32[256,2]{0,1:T(2,128)S(1)}, bf16[3584,2560]{1,0:T(8,128)(2,1)}, bf16[3584,2560]{1,0:T(8,128)(2,1)}, /*index=5*/bf16[2560,3584]{1,0:T(8,128)(2,1)}) %tuple.21, ...), branch_computations={%region_0.0_spmd, %region_1.0_spmd} | conditional | flops 56371445760 | bytes 220205056 | solution.py:866
  285.2 0.8 copy.13.g_ref
  286.0 332.1 %moe4.1 = bf16[256,3584]{1,0:T(8,128)(2,1)} custom-call(bf16[256,3584]{1,0:T(8,128)(2,1)} %get-tuple-element.21.h_ref, s32[256,128]{1,0:T(8,128)} %get-tuple-element.22.dc_ref, f32[256,2]{1,0:T(8,128)} %copy.13.g_ref, bf16[3584,2560]{1,0:T(8,128)(2,1)} %get-tuple-element.24.wg_hbm, bf16[3584,2560]{1,0:T(8,128)(2,1)} %get-tuple-element.25.wu_hbm, ...), custom_call_target="tpu_custom_call" | custom-call | flops 56371445760 | bytes 220200960 | tf_op jit(solution)/shard_map/cond/branch_0_fun/moe4/pallas_call | solution.py:832
  618.2 2.8 copy.17
Async XLA Ops:
  0.0 285.0 %copy-start = (f32[256,2]{0,1:T(2,128)S(1)}, f32[256,2]{0,1:T(2,128)}, u32[]{:S(2)}) copy-start(f32[256,2]{0,1:T(2,128)} %param.14) | copy-start | bytes 6148

commit v5 on v4

--- a/solution.py
+++ b/solution.py
@@ -263,13 +263,18 @@
         pt = lax.rem(t + dt, ntp)
         return pc, pt, pc * ntp + pt
 
-    def out_copy(j, dc, dt):
+    early = 1024
+    cuts = [(0, 0, early), (0, early, hd)] + [(j, 0, hd) for j in range(1, NCH)]
+
+    def out_copy(n, dc, dt):
         pc, pt, e = peer(dc, dt)
-        return rcopy(send.at[j, blk(e)], recv.at[j, blk(self_e)], ssem.at[j, e], rsem.at[j, self_e], d, pc, pt)
-
-    def in_copy(j, dc, dt):
+        j, lo, hi = cuts[n]
+        return rcopy(send.at[j, blk(e), lo:hi], recv.at[j, blk(self_e), lo:hi], ssem.at[n, e], rsem.at[n, self_e], d, pc, pt)
+
+    def in_copy(n, dc, dt):
         pc, pt, e = peer(dc, dt)
-        return rcopy(send.at[j, blk(e)], recv.at[j, blk(e)], ssem.at[j, e], rsem.at[j, e], d, pc, pt)
+        j, lo, hi = cuts[n]
+        return rcopy(send.at[j, blk(e), lo:hi], recv.at[j, blk(e), lo:hi], ssem.at[n, e], rsem.at[n, e], d, pc, pt)
 
     def home_copy(j, dc, dt):
         pc, pt, e = peer(dc, dt)
@@ -299,11 +304,10 @@
         for s in range(2):
             w2_copy(jnp.int32(s)).start()
 
-    def dispatch():
-        for i in range(2):
-            rcopy(xs.at[t_y, half(i)], xs.at[t_y, half(i)], fx_s.at[i], fx_r.at[i], d, c, t_c).wait_send()
+    def dispatch(ns):
         codes = code_ref[...].astype(F32).T.astype(jnp.int32)
-        for j in range(NCH):
+        for n in ns:
+            j, lo, hi = cuts[n]
             ri = lax.broadcasted_iota(jnp.int32, (rows, rb), 0) + j * rows
             sel = (jnp.where(ri == codes[0:1, :], 1.0, 0.0) + jnp.where(ri == codes[1:2, :], 1.0, 0.0)).astype(BF)
 
@@ -312,10 +316,10 @@
                 send[j, :, cols] = dot(sel, h_ref[:, cols]).astype(BF)
                 return 0
 
-            lax.fori_loop(0, nc, pick, 0)
+            lax.fori_loop(lo // 512, hi // 512, pick, 0)
             for dc, dt in peers:
-                out_copy(j, dc, dt).start()
-            recv[j, blk(self_e), :] = send[j, blk(self_e), :]
+                out_copy(n, dc, dt).start()
+            recv[j, blk(self_e), lo:hi] = send[j, blk(self_e), lo:hi]
 
     cw = seg // 2
 
@@ -442,29 +446,36 @@
     def finish_rows():
         for cc in range(ncp):
             x_copy(cc, True, 0).wait_recv()
-        x_copy(far, True, 1).wait_recv()
-
-        @pl.when(c == 0)
-        def _():
-            x_copy(2, True, 1).wait_recv()
-
-        @pl.when(c == ncp - 1)
-        def _():
-            x_copy(ncp - 3, True, 1).wait_recv()
-
-        @pl.when(c > 0)
-        def _():
-            up2_copy(c_dn, c_dn).wait_recv()
-
-        @pl.when(c < ncp - 1)
-        def _():
-            dn2_copy(c_up, c_up).wait_recv()
         loads[4].wait()
         for j in range(heads):
             o_copy(j).wait_recv()
-        lax.fori_loop(0, nc, give, 0)
-        lax.fori_loop(0, nc, keep, 0)
-        dispatch()
+        for i in range(2):
+            rcopy(xs.at[t_y, half(i)], xs.at[t_y, half(i)], fx_s.at[i], fx_r.at[i], d, c, t_c).wait_send()
+        ahead = early // 512
+        lax.fori_loop(0, ahead + 1, give, 0)
+        lax.fori_loop(0, ahead, keep, 0)
+        dispatch([0])
+
+        x_copy(far, True, 1).wait_recv()
+
+        @pl.when(c == 0)
+        def _():
+            x_copy(2, True, 1).wait_recv()
+
+        @pl.when(c == ncp - 1)
+        def _():
+            x_copy(ncp - 3, True, 1).wait_recv()
+
+        @pl.when(c > 0)
+        def _():
+            up2_copy(c_dn, c_dn).wait_recv()
+
+        @pl.when(c < ncp - 1)
+        def _():
+            dn2_copy(c_up, c_up).wait_recv()
+        lax.fori_loop(ahead + 1, nc, give, 0)
+        lax.fori_loop(ahead, nc, keep, 0)
+        dispatch(range(1, len(cuts)))
 
     nc = hd // 512
     def p_copy(i):
@@ -497,8 +508,10 @@
     finish_rows()
 
     for s in range(NCH):
-        for dc, dt in peers:
-            in_copy(s, dc, dt).wait_recv()
+        for n in range(len(cuts)):
+            if cuts[n][0] == s:
+                for dc, dt in peers:
+                    in_copy(n, dc, dt).wait_recv()
 
         def up(i, _):
             for cp_ in w1_copies(i):
@@ -622,8 +635,10 @@
         p_copy(i).wait_send()
     for j in range(NCH):
         for dc, dt in peers:
-            out_copy(j, dc, dt).wait_send()
             home_copy(j, dc, dt).wait_send()
+    for n in range(len(cuts)):
+        for dc, dt in peers:
+            out_copy(n, dc, dt).wait_send()
 
 
 def layer(x, wq, wk, wv, wo, idx, gates, wg, wu, wd, *, nd, ncp, ntp, cid):
@@ -654,7 +669,7 @@
             dma((ncp, 12)), dma((ncp, 12)), dma((2,)), dma((2,)), dma((ncp, 2)), dma((ncp, 2)),
             dma((ncp, 2)), dma((ncp, 2)), dma((ncp, 2)), dma((ncp, 2)), dma(()), dma(()), dma((2,)), dma((2,)), dma((heads,)), dma((heads,)),
             dma((hd // 512,)), dma((hd // 512,)), dma((n_all - 1,)), dma((n_all,)),
-            dma((NCH, ne)), dma((NCH, ne)), dma((NCH, ne)), dma((NCH, ne)), dma((2, 2)), dma((2,)),
+            dma((NCH + 1, ne)), dma((NCH + 1, ne)), dma((NCH, ne)), dma((NCH, ne)), dma((2, 2)), dma((2,)),
         ],
         compiler_params=pltpu.CompilerParams(collective_id=cid, has_side_effects=True, vmem_limit_bytes=VMEM_LIMIT),
         name="layer",

time: 622 us -> 617 us (level)
    pallas_call x1, Pallas kernels: 283 us -> 276 us  [layer(): pl.pallas_call(functools.partial(layer_kernel, nd=nd, ncp=ncp, ntp=ntp, s...]
where the time goes in v5:
time: 617 us; the launch traced here: 614 us
  Pallas kernels  609 us (99%)
    pallas_call x1, Pallas kernels, moe(): pl.pallas_call(functools.partial(moe_kernel, ncp=ncp, ntp=ntp, nch=nch, f...  332 us
    pallas_call x1, Pallas kernels, layer(): pl.pallas_call(functools.partial(layer_kernel, nd=nd, ncp=ncp, ntp=ntp, s...  276 us

profile of v5, /device:TPU:9, one launch (start us, length us, event | category | flops | bytes accessed | tf_op | source)
XLA Modules:
  0.0 614.5 jit_solution(13427097443091384991)
XLA Ops:
  0.0 0.0 copy-start
  0.0 276.4 %layer.1 = (bf16[256,3584]{1,0:T(8,128)(2,1)}, bf16[256,3584]{1,0:T(8,128)(2,1)}, s32[256,128]{1,0:T(8,128)}, f32[8,128]{1,0:T(8,128)}) custom-call(bf16[256,3584]{1,0:T(8,128)(2,1)} %x_hbm.1, bf16[3584,896]{1,0:T(8,128)(2,1)} %wq_hbm.1, bf16[3584,128]{1,0:T(8,128)(2,1)} %wk_hbm.1, bf16[3584,128]{1,0:T(8,128)(2,1)} %wv_hbm.1, bf16[896,3584]{1,0:T(8,128)(2,1)} %wo_hbm.1, ...), custom_call_target="tpu_custom_call" | custom-call | flops 60000002048 | bytes 30000000 | tf_op jit(solution)/shard_map/layer/pallas_call | solution.py:657
  276.4 1.2 slice.3
  278.2 0.0 copy-done
  278.2 333.4 %conditional.1 = (bf16[256,3584]{1,0:T(8,128)(2,1)}) conditional(s32[]{:T(128)} %bitcast.5, (bf16[256,3584]{1,0:T(8,128)(2,1)}, s32[256,128]{1,0:T(8,128)}, f32[256,2]{0,1:T(2,128)S(1)}, bf16[3584,2560]{1,0:T(8,128)(2,1)}, bf16[3584,2560]{1,0:T(8,128)(2,1)}, /*index=5*/bf16[2560,3584]{1,0:T(8,128)(2,1)}) %tuple.21, ...), branch_computations={%region_0.0_spmd, %region_1.0_spmd} | conditional | flops 56371445760 | bytes 220205056 | solution.py:881
  278.5 0.8 copy.13.g_ref
  279.3 332.3 %moe4.1 = bf16[256,3584]{1,0:T(8,128)(2,1)} custom-call(bf16[256,3584]{1,0:T(8,128)(2,1)} %get-tuple-element.21.h_ref, s32[256,128]{1,0:T(8,128)} %get-tuple-element.22.dc_ref, f32[256,2]{1,0:T(8,128)} %copy.13.g_ref, bf16[3584,2560]{1,0:T(8,128)(2,1)} %get-tuple-element.24.wg_hbm, bf16[3584,2560]{1,0:T(8,128)(2,1)} %get-tuple-element.25.wu_hbm, ...), custom_call_target="tpu_custom_call" | custom-call | flops 56371445760 | bytes 220200960 | tf_op jit(solution)/shard_map/cond/branch_0_fun/moe4/pallas_call | solution.py:847
  611.6 2.8 copy.17
Async XLA Ops:
  0.0 278.2 %copy-start = (f32[256,2]{0,1:T(2,128)S(1)}, f32[256,2]{0,1:T(2,128)}, u32[]{:S(2)}) copy-start(f32[256,2]{0,1:T(2,128)} %param.14) | copy-start | bytes 6148

commit v6 on v5

--- a/solution.py
+++ b/solution.py
@@ -438,7 +438,7 @@
     kv_wait(0)
     wo_first(1)
     kv_wait(1)
-    points = [(4, wo_cross), (5, lambda: wo_near(1)), (13, wo_far), (20, lambda: wo_ends(1))]
+    points = [(4, wo_cross), (5, lambda: wo_near(1)), (13, wo_far), (26, lambda: wo_ends(1))]
     done = heads * (other + 1) // 2
     attend(1, other, [(stop, stop <= done, point) for stop, point in points])
     attend(0, mine, [(jnp.maximum(stop - done, 0), stop > done, point) for stop, point in points])

time: 617 us -> 618 us (level)
  no operation moved by 1% of the time
where the time goes in v6:
time: 618 us; the launch traced here: 614 us
  Pallas kernels  609 us (99%)
    pallas_call x1, Pallas kernels, moe(): pl.pallas_call(functools.partial(moe_kernel, ncp=ncp, ntp=ntp, nch=nch, f...  332 us
    pallas_call x1, Pallas kernels, layer(): pl.pallas_call(functools.partial(layer_kernel, nd=nd, ncp=ncp, ntp=ntp, s...  276 us

profile of v6, /device:TPU:9, one launch (start us, length us, event | category | flops | bytes accessed | tf_op | source)
XLA Modules:
  0.0 614.5 jit_solution(4913575801079186555)
XLA Ops:
  0.0 0.0 copy-start
  0.0 276.4 %layer.1 = (bf16[256,3584]{1,0:T(8,128)(2,1)}, bf16[256,3584]{1,0:T(8,128)(2,1)}, s32[256,128]{1,0:T(8,128)}, f32[8,128]{1,0:T(8,128)}) custom-call(bf16[256,3584]{1,0:T(8,128)(2,1)} %x_hbm.1, bf16[3584,896]{1,0:T(8,128)(2,1)} %wq_hbm.1, bf16[3584,128]{1,0:T(8,128)(2,1)} %wk_hbm.1, bf16[3584,128]{1,0:T(8,128)(2,1)} %wv_hbm.1, bf16[896,3584]{1,0:T(8,128)(2,1)} %wo_hbm.1, ...), custom_call_target="tpu_custom_call" | custom-call | flops 60000002048 | bytes 30000000 | tf_op jit(solution)/shard_map/layer/pallas_call | solution.py:657
  276.4 1.2 slice.3
  278.2 0.0 copy-done
  278.3 333.4 %conditional.1 = (bf16[256,3584]{1,0:T(8,128)(2,1)}) conditional(s32[]{:T(128)} %bitcast.5, (bf16[256,3584]{1,0:T(8,128)(2,1)}, s32[256,128]{1,0:T(8,128)}, f32[256,2]{0,1:T(2,128)S(1)}, bf16[3584,2560]{1,0:T(8,128)(2,1)}, bf16[3584,2560]{1,0:T(8,128)(2,1)}, /*index=5*/bf16[2560,3584]{1,0:T(8,128)(2,1)}) %tuple.21, ...), branch_computations={%region_0.0_spmd, %region_1.0_spmd} | conditional | flops 56371445760 | bytes 220205056 | solution.py:881
  278.5 0.8 copy.13.g_ref
  279.3 332.3 %moe4.1 = bf16[256,3584]{1,0:T(8,128)(2,1)} custom-call(bf16[256,3584]{1,0:T(8,128)(2,1)} %get-tuple-element.21.h_ref, s32[256,128]{1,0:T(8,128)} %get-tuple-element.22.dc_ref, f32[256,2]{1,0:T(8,128)} %copy.13.g_ref, bf16[3584,2560]{1,0:T(8,128)(2,1)} %get-tuple-element.24.wg_hbm, bf16[3584,2560]{1,0:T(8,128)(2,1)} %get-tuple-element.25.wu_hbm, ...), custom_call_target="tpu_custom_call" | custom-call | flops 56371445760 | bytes 220200960 | tf_op jit(solution)/shard_map/cond/branch_0_fun/moe4/pallas_call | solution.py:847
  611.6 2.8 copy.17
Async XLA Ops:
  0.0 278.2 %copy-start = (f32[256,2]{0,1:T(2,128)S(1)}, f32[256,2]{0,1:T(2,128)}, u32[]{:S(2)}) copy-start(f32[256,2]{0,1:T(2,128)} %param.14) | copy-start | bytes 6148
